TPU v7x, 8 devices: a whole 2x2x1 slice. The times are simulated.
8 devices in a mesh: dp: 1 (over z), sp: 8 (over y, x, core).
Axes of the slice: x: 2, y: 2, z: 1, core: 2. Of those that a mesh axis runs over, the one named last changes fastest.
Arguments:
- hidden: bfloat16 [32, 7168], P('dp')
- ckv_cache: bfloat16 [32, 16384, 512], P('dp', 'sp')
- kpe_cache: bfloat16 [32, 16384, 64], P('dp', 'sp')
- cache_len: int32 [32], P('dp')
- w_dq: bfloat16 [7168, 1536], replicated
- q_gain: bfloat16 [1536], replicated
- w_uq: bfloat16 [1536, 12288], replicated
- w_dkv: bfloat16 [7168, 576], replicated
- kv_gain: bfloat16 [512], replicated
- w_uk: bfloat16 [64, 128, 512], replicated
- w_uv: bfloat16 [64, 128, 512], replicated
- w_out: bfloat16 [8192, 7168], replicated
Outputs:
- output 1: bfloat16 [32, 7168], P('dp')
- output 2: bfloat16 [32, 16384, 512], P('dp', 'sp')
- output 3: bfloat16 [32, 16384, 64], P('dp', 'sp')
- output 4: bfloat16 [32, 576], P('dp')
All inputs are finite; a program needn't handle non-finite values.
Results may differ from a plain program's by a relative error of at most 0.0112965.
Values sent between devices are 32-bit elements.
A program may use at most 1.5 GiB of HBM per device.

v0:
```python
import jax
import jax.numpy as jnp
from jax import lax
from jax.sharding import PartitionSpec as P

EPS = 1e-6
ROPE_THETA = 10000.0
NEG_FILL = -1e30


def rms_norm(vector, norm_gain):
    mean_sq = jnp.mean(vector * vector, axis=-1, keepdims=True)
    return vector * lax.rsqrt(mean_sq + EPS) * norm_gain.astype(jnp.float32)


def rope_tables(cache_len, rope_dim):
    inv_freq = jnp.power(ROPE_THETA, -2.0 * jnp.arange(rope_dim // 2, dtype=jnp.float32) / rope_dim)
    rope_angle = cache_len.astype(jnp.float32)[:, None] * inv_freq[None, :]
    return jnp.cos(rope_angle), jnp.sin(rope_angle)


def rotate(vector, cos_t, sin_t):
    half_dim = vector.shape[-1] // 2
    first_half = vector[..., :half_dim]
    second_half = vector[..., half_dim:]
    return jnp.concatenate([first_half * cos_t - second_half * sin_t, second_half * cos_t + first_half * sin_t], axis=-1)


def project_token(hidden, cache_len, w_dq, q_gain, w_uq, w_dkv, kv_gain, w_uk):
    n_seqs = hidden.shape[0]
    n_heads, nope_dim, value_a7 = w_uk.shape
    qk_dim = w_uq.shape[1] // n_heads
    cq_raw = jnp.dot(hidden, w_dq, preferred_element_type=jnp.float32)
    c_q = rms_norm(cq_raw, q_gain).astype(jnp.bfloat16)
    q_full = jnp.dot(c_q, w_uq, preferred_element_type=jnp.float32).astype(jnp.bfloat16)
    q_full = q_full.reshape(n_seqs, n_heads, qk_dim)
    cos_t, sin_t = rope_tables(cache_len, qk_dim - nope_dim)
    q_pe = rotate(q_full[:, :, nope_dim:].astype(jnp.float32), cos_t[:, None, :], sin_t[:, None, :]).astype(jnp.bfloat16)
    q_lat = jnp.einsum('bhn,hnc->bhc', q_full[:, :, :nope_dim], w_uk, preferred_element_type=jnp.float32).astype(jnp.bfloat16)
    kv_raw = jnp.dot(hidden, w_dkv, preferred_element_type=jnp.float32)
    c_kv = rms_norm(kv_raw[:, :value_a7], kv_gain)
    k_pe = rotate(kv_raw[:, value_a7:], cos_t, sin_t)
    kv_new = jnp.concatenate([c_kv, k_pe], axis=-1).astype(jnp.bfloat16)
    return q_lat, q_pe, kv_new


def local_terms(q_lat, q_pe, ckv_blk, kpe_blk, positions, cache_len, score_scale):
    scores = jnp.einsum('bhc,btc->bht', q_lat, ckv_blk, preferred_element_type=jnp.float32)
    scores = scores + jnp.einsum('bhr,btr->bht', q_pe, kpe_blk, preferred_element_type=jnp.float32)
    is_valid = positions[:, None, :] <= cache_len[:, None, None]
    scores = jnp.where(is_valid, scores * score_scale, NEG_FILL)
    row_peak = jnp.max(scores, axis=-1, keepdims=True)
    weights = jnp.exp(scores - row_peak)
    row_denom = jnp.sum(weights, axis=-1, keepdims=True)
    lat_sum = jnp.einsum('bht,btc->bhc', weights.astype(jnp.bfloat16), ckv_blk, preferred_element_type=jnp.float32)
    return row_peak, row_denom, lat_sum


def output_proj(o_lat, w_uv, w_out):
    n_seqs = o_lat.shape[0]
    o_heads = jnp.einsum('bhc,hvc->bhv', o_lat, w_uv, preferred_element_type=jnp.float32).astype(jnp.bfloat16)
    return jnp.dot(o_heads.reshape(n_seqs, -1), w_out, preferred_element_type=jnp.float32).astype(jnp.bfloat16)


def solution(mesh):
    def local_step(hidden, ckv_blk, kpe_blk, cache_len, w_dq, q_gain, w_uq, w_dkv, kv_gain, w_uk, w_uv, w_out):
        shard_len = ckv_blk.shape[1]
        value_a7 = ckv_blk.shape[2]
        score_scale = (w_uk.shape[1] + kpe_blk.shape[2]) ** -0.5
        q_lat, q_pe, kv_new = project_token(hidden, cache_len, w_dq, q_gain, w_uq, w_dkv, kv_gain, w_uk)
        positions = lax.axis_index('sp') * shard_len + lax.broadcasted_iota(jnp.int32, (1, shard_len), 1)
        new_slot = (positions == cache_len[:, None])[:, :, None]
        ckv_out = jnp.where(new_slot, kv_new[:, None, :value_a7], ckv_blk)
        kpe_out = jnp.where(new_slot, kv_new[:, None, value_a7:], kpe_blk)
        row_peak, row_denom, lat_sum = local_terms(q_lat, q_pe, ckv_out, kpe_out, positions, cache_len, score_scale)
        local_stats = jnp.concatenate([row_peak, row_denom, lat_sum], axis=-1)
        gathered = lax.all_gather(local_stats, 'sp')
        all_peaks = gathered[..., :1]
        factor = jnp.exp(all_peaks - jnp.max(all_peaks, axis=0))
        weight_total = jnp.sum(factor * gathered[..., 1:2], axis=0)
        o_lat = (jnp.sum(factor * gathered[..., 2:], axis=0) / weight_total).astype(jnp.bfloat16)
        out = output_proj(o_lat, w_uv, w_out)
        return out, ckv_out, kpe_out, kv_new

    cache_spec = P('dp', 'sp', None)
    return jax.shard_map(local_step, mesh=mesh, in_specs=(P('dp', None), cache_spec, cache_spec, P('dp'), P(), P(), P(), P(), P(), P(), P(), P()), out_specs=(P('dp', None), cache_spec, cache_spec, P('dp', None)), check_vma=False)
```

profile of v0, /device:TPU:0, one launch (start us, length us, event | category | flops | bytes accessed | tf_op | source)
XLA Modules:
  0.0 556.6 jit_solution(12031413808528398390)
XLA Ops:
  7.2 0.7 convert_element_type.41
  8.0 0.2 copy-done
  8.2 9.3 %multiply_reduce_fusion = (f32[32]{0:T(128)S(1)}, f32[32,1536]{1,0:T(8,128)S(1)}) fusion(bf16[32,7168]{1,0:T(8,128)(2,1)S(1)} %copy-done, bf16[7168,1536]{1,0:T(8,128)(2,1)} %param.16), kind=kOutput, calls=%fused_computation.35 | convolution fusion | flops 704741376 | bytes 22675584 | tf_op jit(solution)/shard_map/dot_general | solution.py:33
  17.6 15.2 %convolution_convert_fusion = bf16[32,12288]{1,0:T(8,128)(2,1)S(1)} fusion(bf16[1536,12288]{1,0:T(8,128)(2,1)} %param.18, f32[32,1536]{1,0:T(8,128)S(1)} %get-tuple-element.17, f32[1536]{0:T(1024)S(1)} %convert_element_type.41, f32[32]{0:T(128)S(1)} %add_rsqrt_fusion.1), kind=kOutput, calls=%fused_computation.7 | convolution fusion | flops 1208500224 | bytes 38738048 | tf_op jit(solution)/shard_map/dot_general | solution.py:35
  32.8 1.2 reshape.157
  34.0 0.1 slice.49
  34.1 0.1 slice_convert_fusion
  34.2 5.8 %fusion.33 = f32[32,576]{1,0:T(8,128)S(1)} fusion(bf16[32,7168]{1,0:T(8,128)(2,1)S(1)} %copy-done, bf16[7168,576]{0,1:T(8,128)(2,1)} %param.19), kind=kOutput, calls=%fused_computation.60 | convolution fusion | flops 264241152 | bytes 8790016 | tf_op jit(solution)/shard_map/dot_general | solution.py:40
  40.0 0.1 multiply_reduce_fusion.1
  40.2 0.1 broadcast_compare_fusion.1
  40.4 0.1 multiply_cosine_fusion
  40.6 6.2 %convert_bitcast_fusion = bf16[32,64,512]{2,0,1:T(8,128)(2,1)} fusion(bf16[64,128,512]{2,1,0:T(8,128)(2,1)} %param.21, bf16[32,64,128]{2,1,0:T(8,128)(2,1)S(1)} %slice.49), kind=kOutput, calls=%fused_computation.21 | convolution fusion | flops 269484032 | bytes 11010048 | tf_op jit(solution)/shard_map/bhn,hnc->bhc/dot_general | solution.py:39
  46.8 7.5 %broadcast_select_fusion.1 = bf16[32,2048,64]{1,2,0:T(8,128)(2,1)} fusion(bf16[32,2048,64]{1,2,0:T(8,128)(2,1)} %param.14, pred[32,2048]{1,0:T(8,128)(4,1)S(1)} %get-tuple-element.11, bf16[32,64]{1,0:T(8,128)(2,1)S(1)} %pad_maximum_fusion.2), kind=kLoop, calls=%fused_computation.12 | loop fusion | flops 4194304 | bytes 16846848 | tf_op jit(solution)/shard_map/jit(_where)/select_n | solution.py:74
  54.3 44.4 %broadcast_select_fusion = bf16[32,2048,512]{2,1,0:T(8,128)(2,1)} fusion(bf16[32,2048,512]{2,1,0:T(8,128)(2,1)} %param.13, pred[32,2048]{1,0:T(8,128)(4,1)S(1)} %get-tuple-element.11, bf16[32,512]{1,0:T(8,128)(2,1)S(1)} %multiply_convert_fusion.2), kind=kLoop, calls=%fused_computation.2 | loop fusion | flops 33554432 | bytes 134316032 | tf_op jit(solution)/shard_map/jit(_where)/select_n | solution.py:73
  98.7 0.5 subtract_convert_fusion
  99.3 11.6 %fusion.21 = f32[32,64,2048]{2,1,0:T(8,128)} fusion(bf16[32,2048,64]{1,2,0:T(8,128)(2,1)} %broadcast_select_fusion.1, bf16[32,64,32]{2,1,0:T(8,128)(2,1)S(1)} %get-tuple-element.7, bf16[32,64,32]{2,1,0:T(8,128)(2,1)S(1)} %get-tuple-element.6), kind=kOutput, calls=%fused_computation.29 | convolution fusion | flops 537395200 | bytes 25427968 | tf_op jit(solution)/shard_map/bhr,btr->bht/dot_general | solution.py:49
  110.9 36.1 %fusion.6 = (f32[32,64]{1,0:T(8,128)S(1)}, f32[32,64,2048]{2,1,0:T(8,128)}) fusion(f32[32,64,2048]{2,1,0:T(8,128)} %fusion.21, pred[32,2048]{1,0:T(8,128)(4,1)S(1)} %get-tuple-element.10, bf16[32,2048,512]{2,1,0:T(8,128)(2,1)} %broadcast_select_fusion, bf16[32,64,512]{2,0,1:T(8,128)(2,1)S(1)} %copy-done.2), kind=kOutput, calls=%fused_computation.10 | convolution fusion | flops 4311742464 | bytes 102834176 | tf_op jit(solution)/shard_map/bhc,btc->bht/dot_general | solution.py:48
  147.0 12.1 %fusion.2 = f32[32,64]{1,0:T(8,128)S(1)} fusion(f32[32,64]{1,0:T(8,128)S(1)} %get-tuple-element.18, f32[32,64,2048]{2,1,0:T(8,128)} %get-tuple-element.19, f32[32,64,2048]{2,1,0:T(8,128)} %fusion.21, pred[32,2048]{1,0:T(8,128)(4,1)S(1)} %get-tuple-element.10), kind=kLoop, calls=%fused_computation.6 | loop fusion | flops 20969472 | bytes 33636352 | tf_op jit(solution)/shard_map/reduce_sum | solution.py:54
  159.1 35.4 %fusion.3 = f32[32,64,512]{2,1,0:T(8,128)} fusion(bf16[32,2048,512]{2,1,0:T(8,128)(2,1)} %broadcast_select_fusion, f32[32,64]{1,0:T(8,128)S(1)} %get-tuple-element.18, f32[32,64,2048]{2,1,0:T(8,128)} %get-tuple-element.19, f32[32,64,2048]{2,1,0:T(8,128)} %fusion.21, pred[32,2048]{1,0:T(8,128)(4,1)S(1)} %get-tuple-element.10), kind=kOutput, calls=%fused_computation.8 | convolution fusion | flops 4315938816 | bytes 104931328 | tf_op jit(solution)/shard_map/bht,btc->bhc/dot_general | solution.py:55
  194.5 0.4 copy.24
  194.9 0.4 copy.23
  195.3 6.5 %pad_maximum_fusion = f32[32,64,514]{2,1,0:T(8,128)} fusion(f32[32,64,512]{2,1,0:T(8,128)} %fusion.3, f32[32,64,1]{2,1,0:T(8,128)S(1)} %copy.24, f32[32,64,1]{2,1,0:T(8,128)S(1)} %copy.23), kind=kLoop, calls=%fused_computation.15 | loop fusion | flops 2105344 | bytes 8421376 | tf_op jit(solution)/shard_map/concatenate | solution.py:76
  201.8 0.7 pad_maximum_fusion.1
  202.5 193.8 %all-gather.3.cloned.1.call-done = f32[256,64,514]{2,1,0:T(8,128)} async-done(((f32[32,64,514]{2,1,0:T(8,128)}), f32[256,64,514]{2,1,0:T(8,128)}) %all-gather.3.cloned.1.call-update) | async-done | bytes 33685520 | tf_op jit(solution)/shard_map/all_gather | solution.py:77
  396.3 70.8 %copy.25 = f32[256,64,514]{1,0,2:T(8,128)} copy(f32[256,64,514]{2,1,0:T(8,128)} %all-gather.3.cloned.1.call-done) | data formatting | bytes 67371008 | tf_op jit(solution)/shard_map/all_gather | solution.py:77
  467.1 0.9 slice_reduce_fusion
  468.0 1.0 fusion.26
  469.0 25.3 %fusion = f32[32,64,512]{1,0,2:T(8,128)} fusion(f32[8,32,64,514]{2,1,0,3:T(8,128)} %bitcast.3, f32[8,32,64]{2,1,0:T(8,128)S(1)} %get-tuple-element.5), kind=kLoop, calls=%fused_computation.1 | loop fusion | flops 15728640 | bytes 37814272 | tf_op jit(solution)/shard_map/reduce_sum | solution.py:81
  494.3 6.8 %copy.29 = f32[32,64,512]{2,1,0:T(8,128)} copy(f32[32,64,512]{1,0,2:T(8,128)} %fusion) | data formatting | bytes 8388608
  501.1 2.6 divide_convert_fusion
  503.7 5.8 %fusion.16 = bf16[64,4,8,128]{3,2,1,0:T(8,128)(2,1)S(1)} fusion(bf16[64,128,512]{2,1,0:T(8,128)(2,1)} %param.22, bf16[32,64,512]{2,1,0:T(8,128)(2,1)S(1)} %divide_convert_fusion), kind=kOutput, calls=%fused_computation.23 | convolution fusion | flops 268697600 | bytes 11010048 | tf_op jit(solution)/shard_map/bhc,hvc->bhv/dot_general | solution.py:61
  509.5 40.3 %convolution_convert_fusion.1 = bf16[32,7168]{1,0:T(8,128)(2,1)} fusion(bf16[8192,7168]{1,0:T(8,128)(2,1)} %param.23, bf16[64,4,8,128]{3,2,1,0:T(8,128)(2,1)S(1)} %fusion.16), kind=kOutput, calls=%fused_computation.14 | convolution fusion | flops 3758325760 | bytes 118423552 | tf_op jit(solution)/shard_map/dot_general | solution.py:62
  (19 shorter events, 0.3 us)
Async XLA Ops:
  7.2 1.0 copy-start
  7.2 389.1 %all-gather.3.cloned.1.call-start = ((), (), s32[]{:S(2)}) async-start(), calls=%async_computation | async-start | bytes 47185920 | tf_op jit(solution)/shard_map/all_gather | solution.py:77
  17.5 16.6 %copy-start.4 = (s32[32]{0:T(128)S(1)}, s32[32]{0:T(128)}, u32[]{:S(2)}) copy-start(s32[32]{0:T(128)} %param.15) | copy-start | bytes 388
  17.6 16.7 %copy-start.3 = (bf16[512]{0:T(512)(128)(2,1)S(1)}, bf16[512]{0:T(512)(128)(2,1)}, u32[]{:S(2)}) copy-start(bf16[512]{0:T(512)(128)(2,1)} %param.20) | copy-start | bytes 3076
  99.3 11.7 %copy-start.2 = (bf16[32,64,512]{2,0,1:T(8,128)(2,1)S(1)}, bf16[32,64,512]{2,0,1:T(8,128)(2,1)}, u32[]{:S(2)}) copy-start(bf16[32,64,512]{2,0,1:T(8,128)(2,1)} %convert_bitcast_fusion) | copy-start | bytes 6291460
  509.5 40.3 %copy-start.1 = (bf16[32,7168]{1,0:T(8,128)(2,1)S(1)}, bf16[32,7168]{1,0:T(8,128)(2,1)}, u32[]{:S(2)}) copy-start(bf16[32,7168]{1,0:T(8,128)(2,1)} %param.12) | copy-start | bytes 1376260
Sparse Core Ops, SparseCore 0:
  201.9 194.3 all-gather.2
where the time goes:
time: 559 us; the launch traced here: 557 us
  waiting for transfers between devices  194 us (35%)
  matrix products  166 us (30%)
  other arithmetic  103 us (18%)
  local copies, waits for them, and re-layouts  80 us (14%)
  between operations  14.2 us (3%)
    all_gather x1, waiting for transfers between devices, local_step(): gathered = lax.all_gather(local_stats, 'sp')  194 us
    all_gather x1, local copies, waits for them, and re-layouts, local_step(): gathered = lax.all_gather(local_stats, 'sp')  70.8 us
    select_n x1, other arithmetic, local_step(): ckv_out = jnp.where(new_slot, kv_new[:, None, :value_a7], ckv_blk)  44.4 us
    dot_general x1, matrix products, output_proj(): jnp.dot(o_heads.reshape(n_seqs, -1), w_out, preferred_element_type=jnp.fl...  40.3 us
    dot_general x1, matrix products, local_terms(): jnp.einsum('bhc,btc->bht', q_lat, ckv_blk, preferred_element_type=jnp.flo...  36.1 us
    dot_general x1, matrix products, local_terms(): jnp.einsum('bht,btc->bhc', weights.astype(jnp.bfloat16), ckv_blk, preferr...  35.4 us
    reduce_sum x1, other arithmetic, local_step(): jnp.sum(factor * gathered[..., 2:], axis=0) / weight_total  25.3 us
    dot_general x1, matrix products, project_token(): jnp.dot(c_q, w_uq, preferred_element_type=jnp.float32).astype(jnp.bfloat16)  15.2 us
  transfers between devices with their start and end apart: 1, of which 1 were waited for; matrix products, arithmetic and copies ran while one was open for 0% of the time, Pallas kernels for 0%

commit v1 on v0

v1 whole, which is shorter than its diff:
```python
import functools

import jax
import jax.numpy as jnp
from jax import lax
from jax.experimental import pallas as pl
from jax.experimental.pallas import tpu as pltpu
from jax.sharding import PartitionSpec as P

EPS = 1e-6
ROPE_THETA = 10000.0
NEG_FILL = -1e30
MESH = pl.DeviceIdType.MESH
VMEM = pl.BlockSpec(memory_space=pltpu.VMEM)
SMEM = pl.BlockSpec(memory_space=pltpu.SMEM)
ANY = pl.BlockSpec(memory_space=pl.ANY)


def rms_norm(vector, norm_gain):
    mean_sq = jnp.mean(vector * vector, axis=-1, keepdims=True)
    return vector * lax.rsqrt(mean_sq + EPS) * norm_gain.astype(jnp.float32)


def rope_tables(cache_len, rope_dim):
    inv_freq = jnp.power(ROPE_THETA, -2.0 * jnp.arange(rope_dim // 2, dtype=jnp.float32) / rope_dim)
    rope_angle = cache_len.astype(jnp.float32)[:, None] * inv_freq[None, :]
    return jnp.cos(rope_angle), jnp.sin(rope_angle)


def rotate(vector, cos_t, sin_t):
    half_dim = vector.shape[-1] // 2
    first_half = vector[..., :half_dim]
    second_half = vector[..., half_dim:]
    return jnp.concatenate([first_half * cos_t - second_half * sin_t, second_half * cos_t + first_half * sin_t], axis=-1)


def project_token(hidden, cache_len, w_dq, q_gain, w_uq, w_dkv, kv_gain, w_uk):
    n_seqs = hidden.shape[0]
    n_heads, nope_dim, value_a7 = w_uk.shape
    qk_dim = w_uq.shape[1] // n_heads
    cq_raw = jnp.dot(hidden, w_dq, preferred_element_type=jnp.float32)
    c_q = rms_norm(cq_raw, q_gain).astype(jnp.bfloat16)
    q_full = jnp.dot(c_q, w_uq, preferred_element_type=jnp.float32).astype(jnp.bfloat16)
    q_full = q_full.reshape(n_seqs, n_heads, qk_dim)
    cos_t, sin_t = rope_tables(cache_len, qk_dim - nope_dim)
    q_pe = rotate(q_full[:, :, nope_dim:].astype(jnp.float32), cos_t[:, None, :], sin_t[:, None, :]).astype(jnp.bfloat16)
    q_lat = jnp.einsum('bhn,hnc->bhc', q_full[:, :, :nope_dim], w_uk, preferred_element_type=jnp.float32).astype(jnp.bfloat16)
    kv_raw = jnp.dot(hidden, w_dkv, preferred_element_type=jnp.float32)
    c_kv = rms_norm(kv_raw[:, :value_a7], kv_gain)
    k_pe = rotate(kv_raw[:, value_a7:], cos_t, sin_t)
    kv_new = jnp.concatenate([c_kv, k_pe], axis=-1).astype(jnp.bfloat16)
    return q_lat, q_pe, kv_new


def attend_kernel(cfg, len_ref, qlat_ref, qpe_ref, ckvn_ref, kpen_ref, ckv_hbm, kpe_hbm, cout_hbm, kout_hbm, o_hbm,
                  cbuf, kbuf, obuf, stats, isem, osem, psem):
    n_seqs, shard_len = ckv_hbm.shape[0], ckv_hbm.shape[1]
    n_heads = stats.shape[0]
    n_buf, lag, chunk = cfg["n_buf"], cfg["lag"], cfg["chunk"]
    base = lax.axis_index('sp') * shard_len

    def copies_in(b, slot):
        return (pltpu.make_async_copy(ckv_hbm.at[b], cbuf.at[slot], isem.at[slot, 0]),
                pltpu.make_async_copy(kpe_hbm.at[b], kbuf.at[slot], isem.at[slot, 1]))

    def copies_out(b, slot):
        return (pltpu.make_async_copy(cbuf.at[slot], cout_hbm.at[b], osem.at[slot, 0]),
                pltpu.make_async_copy(kbuf.at[slot], kout_hbm.at[b], osem.at[slot, 1]))

    def copy_terms(b, side):
        return pltpu.make_async_copy(obuf.at[side], o_hbm.at[:, b], psem.at[side])

    for i in range(n_buf - lag):
        for c in copies_in(i, i):
            c.start()
    stats[...] = jnp.zeros_like(stats)

    def step(b, carry):
        slot = lax.rem(b, n_buf)

        @pl.when(b >= lag)
        def _():
            for c in copies_out(b - lag, lax.rem(b - lag + n_buf, n_buf)):
                c.wait()

        ahead = b - lag + n_buf

        @pl.when(ahead < n_seqs)
        def _():
            for c in copies_in(ahead, lax.rem(ahead, n_buf)):
                c.start()

        for c in copies_in(b, slot):
            c.wait()
        last = len_ref[b] - base

        @pl.when((last >= 0) & (last < shard_len))
        def _():
            r0 = pl.multiple_of((last // 16) * 16, 16)
            rows = cbuf[slot, pl.ds(r0, 16), :].astype(jnp.float32)
            row = lax.broadcasted_iota(jnp.int32, rows.shape, 0)
            cbuf[slot, pl.ds(r0, 16), :] = jnp.where(row == last - r0, ckvn_ref[b].astype(jnp.float32), rows).astype(cbuf.dtype)
            c0 = pl.multiple_of((last // 128) * 128, 128)
            cols = kbuf[slot, :, pl.ds(c0, 128)].astype(jnp.float32)
            lane = lax.broadcasted_iota(jnp.int32, cols.shape, 1)
            fresh = jnp.sum(jnp.where(lane == b, kpen_ref[...].astype(jnp.float32), 0.0), axis=1, keepdims=True)
            kbuf[slot, :, pl.ds(c0, 128)] = jnp.where(lane == last - c0, fresh, cols).astype(kbuf.dtype)

        q_lat, q_pe = qlat_ref[b], qpe_ref[b]
        scores = []
        for t in range(0, shard_len, chunk):
            s = lax.dot_general(q_lat, cbuf[slot, t:t + chunk, :], (((1,), (1,)), ((), ())), preferred_element_type=jnp.float32)
            s = s + jnp.dot(q_pe, kbuf[slot, :, t:t + chunk], preferred_element_type=jnp.float32)
            pos = lax.broadcasted_iota(jnp.int32, (1, chunk), 1) + t
            scores.append(jnp.where(pos <= last, s * cfg["scale"], NEG_FILL))
        peak = functools.reduce(jnp.maximum, [jnp.max(s, axis=1, keepdims=True) for s in scores])
        denom = jnp.zeros_like(peak)
        lat_sum = None
        for k, t in enumerate(range(0, shard_len, chunk)):
            w = jnp.exp(scores[k] - peak)
            denom = denom + jnp.sum(w, axis=1, keepdims=True)
            term = jnp.dot(w.astype(jnp.bfloat16), cbuf[slot, t:t + chunk, :], preferred_element_type=jnp.float32)
            lat_sum = term if lat_sum is None else lat_sum + term
        for c in copies_out(b, slot):
            c.start()
        side = lax.rem(b, 2)

        @pl.when(b >= 2)
        def _():
            copy_terms(b - 2, side).wait()

        obuf[side] = lat_sum.reshape(obuf.shape[1:])
        lane = lax.broadcasted_iota(jnp.int32, stats.shape, 1)
        stats[...] = jnp.where(lane == b, peak, jnp.where(lane == b + 64, denom, stats[...]))
        copy_terms(b, side).start()
        return carry

    lax.fori_loop(0, n_seqs, step, 0)
    for i in range(n_seqs - 2, n_seqs):
        copy_terms(i, i % 2).wait()
    obuf[0, :, :, 0:128] = stats[...].reshape(obuf.shape[1], obuf.shape[2], 128)
    copy_terms(n_seqs, 0).start()
    for i in range(n_seqs - lag, n_seqs):
        for c in copies_out(i, i % n_buf):
            c.wait()
    copy_terms(n_seqs, 0).wait()


def attend(q_lat, q_pe, kv_new, cache_len, ckv_blk, kpe_blk_t, n_dev):
    n_seqs, shard_len, lat_dim = ckv_blk.shape
    rope_dim = kpe_blk_t.shape[1]
    n_heads = q_lat.shape[1]
    cfg = dict(n_buf=8, lag=3, chunk=512, scale=(128 + rope_dim) ** -0.5)
    ckv_new = kv_new[:, :lat_dim].reshape(n_seqs, 1, lat_dim)
    kpe_new_t = jnp.pad(kv_new[:, lat_dim:].T, ((0, 0), (0, 128 - n_seqs)))
    terms_shape = (n_dev, n_seqs + 1, n_heads // n_dev, lat_dim)
    return pl.pallas_call(
        functools.partial(attend_kernel, cfg),
        out_shape=(
            jax.ShapeDtypeStruct(ckv_blk.shape, ckv_blk.dtype),
            jax.ShapeDtypeStruct(kpe_blk_t.shape, kpe_blk_t.dtype),
            jax.ShapeDtypeStruct(terms_shape, jnp.float32),
        ),
        in_specs=[SMEM, VMEM, VMEM, VMEM, VMEM, ANY, ANY],
        out_specs=(ANY, ANY, ANY),
        scratch_shapes=[
            pltpu.VMEM((cfg["n_buf"], shard_len, lat_dim), ckv_blk.dtype),
            pltpu.VMEM((cfg["n_buf"], rope_dim, shard_len), kpe_blk_t.dtype),
            pltpu.VMEM((2, n_dev, n_heads // n_dev, lat_dim), jnp.float32),
            pltpu.VMEM((n_heads, 128), jnp.float32),
            pltpu.SemaphoreType.DMA((cfg["n_buf"], 2)),
            pltpu.SemaphoreType.DMA((cfg["n_buf"], 2)),
            pltpu.SemaphoreType.DMA((2,)),
        ],
        compiler_params=pltpu.CompilerParams(vmem_limit_bytes=56 * 1024 * 1024),
        name="attend",
    )(cache_len, q_lat, q_pe, ckv_new, kpe_new_t, ckv_blk, kpe_blk_t)


def finish_kernel(terms, w_uv, w_out, out_ref, orecv, uv, wo, merged, oheads, psend, precv, isend, irecv, fin, agr, agp,
                  lsem, o_ss, o_rs, p_ss, p_rs, i_ss, i_rs, a_ss, a_rs, f_ss, f_rs):
    n_seqs, width = fin.shape
    heads = uv.shape[0]
    depth = wo.shape[0]
    me = lax.axis_index('sp')
    y, x, c = me // 4, (me // 2) % 2, me % 2

    def device(q, jc):
        return ((y + q // 2) % 2) * 4 + ((x + q % 2) % 2) * 2 + (c + jc) % 2

    def send(src, dst, ss, rs, dev):
        return pltpu.make_async_remote_copy(src_ref=src, dst_ref=dst, send_sem=ss, recv_sem=rs, device_id={'sp': dev}, device_id_type=MESH)

    load_uv = pltpu.make_async_copy(w_uv.at[pl.ds(me * heads, heads)], uv, lsem.at[0])
    load_wo = pltpu.make_async_copy(w_out.at[pl.ds(me * depth, depth)], wo, lsem.at[1])
    load_own = pltpu.make_async_copy(terms.at[me], orecv.at[0], lsem.at[2])
    load_own.start()
    load_uv.start()
    load_wo.start()

    others = [(q, jc) for q in (3, 1, 2, 0) for jc in (0, 1) if (q, jc) != (0, 0)]
    barrier = pltpu.get_barrier_semaphore()
    for q, jc in others:
        pl.semaphore_signal(barrier, inc=1, device_id={'sp': device(q, jc)}, device_id_type=MESH)
    pl.semaphore_wait(barrier, len(others))

    o_sends = []
    for q, jc in others:
        j = q * 2 + jc
        o_sends.append(send(terms.at[device(q, jc)], orecv.at[j], o_ss.at[j], o_rs.at[j], device(q, jc)))
        o_sends[-1].start()
    load_own.wait()
    for s in o_sends:
        s.wait_recv()
    stats = [orecv[j, n_seqs, :, 0:128] for j in range(8)]
    peak = functools.reduce(jnp.maximum, stats)
    factors = [jnp.exp(s - peak) for s in stats]
    denoms = [pltpu.roll(s, 64, 1) for s in stats]
    total = functools.reduce(jnp.add, [f * d for f, d in zip(factors, denoms)])
    factors = [f / total for f in factors]
    for b in range(n_seqs):
        acc = None
        for j in range(8):
            t = factors[j][:, b:b + 1] * orecv[j, b]
            acc = t if acc is None else acc + t
        for k in range(merged.shape[0]):
            merged[k, b * heads:(b + 1) * heads, :] = acc[:, k * 128:(k + 1) * 128]
    load_uv.wait()
    for h in range(heads):
        o_lat = jnp.concatenate([merged[k, pl.ds(h, n_seqs, stride=heads), :] for k in range(merged.shape[0])], axis=1).astype(jnp.bfloat16)
        o_h = lax.dot_general(o_lat, uv[h], (((1,), (1,)), ((), ())), preferred_element_type=jnp.float32)
        oheads[:, h * o_h.shape[1]:(h + 1) * o_h.shape[1]] = o_h.astype(jnp.bfloat16)
    load_wo.wait()

    def partial_out(dev):
        cols = pl.ds(pl.multiple_of(dev * width, 128), width)
        return jnp.dot(oheads[...], wo[:, cols], preferred_element_type=jnp.float32)

    waiting = []
    p_sends, i_sends = {}, []
    for q in (3, 1, 2, 0):
        psend[q] = partial_out(device(q, 1))
        p_sends[q] = send(psend.at[q], precv.at[q], p_ss.at[q], p_rs.at[q], device(0, 1))
        for w in waiting:
            w.start()
        waiting = [p_sends[q]]
    mine = None
    for q in (3, 1, 2, 0):
        part = partial_out(device(q, 0))
        for w in waiting:
            w.start()
        waiting = []
        p_sends[q].wait_recv()
        if q:
            isend[q - 1] = part + precv[q]
            i_sends.append(send(isend.at[q - 1], irecv.at[q - 1], i_ss.at[q - 1], i_rs.at[q - 1], device(q, 0)))
            waiting = [i_sends[-1]]
        else:
            mine = part + precv[0]
    for s in i_sends:
        s.wait_recv()
    result = mine + irecv[0] + irecv[1] + irecv[2]
    fin[...] = result
    out_ref[:, pl.ds(pl.multiple_of(me * width, 128), width)] = result.astype(out_ref.dtype)

    a_sends = {q: send(fin, agr.at[q - 1], a_ss.at[q - 1], a_rs.at[q - 1], device(q, 0)) for q in (3, 1, 2)}
    f_sends = {0: send(fin, agp.at[0], f_ss.at[0], f_rs.at[0], device(0, 1))}
    for q in (3, 1, 2):
        a_sends[q].start()
    f_sends[0].start()
    for q in (1, 2, 3):
        f_sends[q] = send(agr.at[q - 1], agp.at[q], f_ss.at[q], f_rs.at[q], device(0, 1))
        a_sends[q].wait_recv()
        f_sends[q].start()
        out_ref[:, pl.ds(pl.multiple_of(device(q, 0) * width, 128), width)] = agr[q - 1].astype(out_ref.dtype)
    for q in range(4):
        f_sends[q].wait_recv()
        out_ref[:, pl.ds(pl.multiple_of(device(q, 1) * width, 128), width)] = agp[q].astype(out_ref.dtype)
    for s in o_sends + list(p_sends.values()) + i_sends + list(a_sends.values()) + list(f_sends.values()):
        s.wait_send()


def finish(terms, w_uv, w_out):
    n_dev, rows, heads, lat_dim = terms.shape
    n_seqs = rows - 1
    d_model = w_out.shape[1]
    depth = w_out.shape[0] // n_dev
    width = d_model // n_dev
    f32 = jnp.float32
    return pl.pallas_call(
        finish_kernel,
        out_shape=jax.ShapeDtypeStruct((n_seqs, d_model), jnp.bfloat16),
        in_specs=[ANY, ANY, ANY],
        out_specs=VMEM,
        scratch_shapes=[
            pltpu.VMEM((n_dev, rows, heads, lat_dim), f32),
            pltpu.VMEM((heads,) + w_uv.shape[1:], w_uv.dtype),
            pltpu.VMEM((depth, d_model), w_out.dtype),
            pltpu.VMEM((lat_dim // 128, n_seqs * heads, 128), f32),
            pltpu.VMEM((n_seqs, depth), jnp.bfloat16),
            pltpu.VMEM((4, n_seqs, width), f32),
            pltpu.VMEM((4, n_seqs, width), f32),
            pltpu.VMEM((3, n_seqs, width), f32),
            pltpu.VMEM((3, n_seqs, width), f32),
            pltpu.VMEM((n_seqs, width), f32),
            pltpu.VMEM((3, n_seqs, width), f32),
            pltpu.VMEM((4, n_seqs, width), f32),
            pltpu.SemaphoreType.DMA((3,)),
            pltpu.SemaphoreType.DMA((8,)),
            pltpu.SemaphoreType.DMA((8,)),
            pltpu.SemaphoreType.DMA((4,)),
            pltpu.SemaphoreType.DMA((4,)),
            pltpu.SemaphoreType.DMA((3,)),
            pltpu.SemaphoreType.DMA((3,)),
            pltpu.SemaphoreType.DMA((3,)),
            pltpu.SemaphoreType.DMA((3,)),
            pltpu.SemaphoreType.DMA((4,)),
            pltpu.SemaphoreType.DMA((4,)),
        ],
        compiler_params=pltpu.CompilerParams(collective_id=0, has_side_effects=True, vmem_limit_bytes=56 * 1024 * 1024),
        name="finish",
    )(terms, w_uv, w_out)


def solution(mesh):
    n_dev = mesh.shape['sp']

    def local_step(hidden, ckv_blk, kpe_blk, cache_len, w_dq, q_gain, w_uq, w_dkv, kv_gain, w_uk, w_uv, w_out):
        q_lat, q_pe, kv_new = project_token(hidden, cache_len, w_dq, q_gain, w_uq, w_dkv, kv_gain, w_uk)
        ckv_out, kpe_out_t, terms = attend(q_lat, q_pe, kv_new, cache_len, ckv_blk, jnp.swapaxes(kpe_blk, 1, 2), n_dev)
        out = finish(terms, w_uv, w_out)
        return out, ckv_out, jnp.swapaxes(kpe_out_t, 1, 2), kv_new

    cache_spec = P('dp', 'sp', None)
    return jax.shard_map(local_step, mesh=mesh, in_specs=(P('dp', None), cache_spec, cache_spec, P('dp'), P(), P(), P(), P(), P(), P(), P(), P()), out_specs=(P('dp', None), cache_spec, cache_spec, P('dp', None)), check_vma=False)
```

time: 559 us -> 175 us (0.31)
  waiting for transfers between devices: 194 us -> 0 us
  matrix products: 166 us -> 35.1 us
  Pallas kernels: 0 us -> 126 us
  other arithmetic: 103 us -> 5.07 us
  local copies, waits for them, and re-layouts: 80 us -> 7.41 us
  between operations: 14.2 us -> 0.75 us
    all_gather x1 -> x0, waiting for transfers between devices: 194 us -> none  [local_step(): gathered = lax.all_gather(local_stats, 'sp')]
    dot_general x5 -> x0, matrix products: 129 us -> none  [the longest x1 40.3 us: output_proj(): jnp.dot(o_heads.reshape(n_seqs, -1), w_out, preferred_element_type=jnp.fl...]
    pallas_call x0 -> x2, Pallas kernels: none -> 126 us  [the longest x1 72.1 us: finish(): pl.pallas_call(finish_kernel, out_shape=jax.ShapeDtypeStruct((n_seqs, d_m...]
    all_gather x1 -> x0, local copies, waits for them, and re-layouts: 70.8 us -> none  [local_step(): gathered = lax.all_gather(local_stats, 'sp')]
    select_n x2 -> x0, other arithmetic: 51.9 us -> none  [the longest x1 44.4 us: local_step(): ckv_out = jnp.where(new_slot, kv_new[:, None, :value_a7], ckv_blk)]
    reduce_sum x3 -> x0, other arithmetic: 38.4 us -> none  [the longest x1 25.3 us: local_step(): jnp.sum(factor * gathered[..., 2:], axis=0) / weight_total]
  transfers between devices with their start and end apart: 1 -> 0, of which waited for: 1 -> 0; matrix products, arithmetic and copies ran while one was open for 0% -> 0% of each run, Pallas kernels for 0% -> 0%
where the time goes in v1:
time: 175 us; the launch traced here: 174 us
  Pallas kernels  126 us (72%)
  matrix products  35.1 us (20%)
  local copies, waits for them, and re-layouts  7.41 us (4%)
  other arithmetic  5.07 us (3%)
    pallas_call x1, Pallas kernels, finish(): pl.pallas_call(finish_kernel, out_shape=jax.ShapeDtypeStruct((n_seqs, d_m...  72.1 us
    pallas_call x1, Pallas kernels, attend(): pl.pallas_call(functools.partial(attend_kernel, cfg), out_shape=(jax.Shap...  54 us
    dot_general x1, matrix products, project_token(): jnp.dot(c_q, w_uq, preferred_element_type=jnp.float32).astype(jnp.bfloat16)  15.2 us
    dot_general x1, matrix products, project_token(): cq_raw = jnp.dot(hidden, w_dq, preferred_element_type=jnp.float32)  9.31 us
    dot_general x1, matrix products, project_token(): kv_raw = jnp.dot(hidden, w_dkv, preferred_element_type=jnp.float32)  5.79 us
    dot_general x1, matrix products, project_token(): jnp.einsum('bhn,hnc->bhc', q_full[:, :, :nope_dim], w_uk, preferred_eleme...  4.82 us

profile of v1, /device:TPU:0, one launch (start us, length us, event | category | flops | bytes accessed | tf_op | source)
XLA Modules:
  0.0 174.4 jit_solution(17351059576676788745)
XLA Ops:
  0.6 0.0 copy-start
  0.6 0.7 convert_element_type.33
  1.4 0.7 convert_element_type.34
  2.1 0.7 convert_element_type.27
  2.7 5.8 %fusion.6 = f32[32,576]{1,0:T(8,128)S(1)} fusion(bf16[32,7168]{1,0:T(8,128)(2,1)S(1)} %copy-done, bf16[7168,576]{0,1:T(8,128)(2,1)} %param.19), kind=kOutput, calls=%fused_computation.25 | convolution fusion | flops 264241152 | bytes 8790016 | tf_op jit(solution)/shard_map/dot_general | solution.py:48
  8.5 0.1 multiply_reduce_fusion.1
  8.7 0.1 fusion.13
  8.8 0.1 multiply_convert_fusion.2
  8.8 0.1 fusion.5
  8.9 0.1 copy.34
  9.0 0.1 copy.33
  9.1 0.2 subtract_convert_fusion.1
  9.2 0.1 copy.27
  9.3 0.1 copy.31
  9.4 0.1 copy.32
  9.5 0.7 pad_maximum_fusion.1
  10.2 0.6 pad.4.kpen_ref
  10.8 0.1 copy.26
  10.9 0.7 copy.30.ckvn_ref
  11.6 9.3 %multiply_reduce_fusion = (f32[32]{0:T(128)S(1)}, f32[32,1536]{1,0:T(8,128)S(1)}) fusion(bf16[32,7168]{1,0:T(8,128)(2,1)S(1)} %copy-done, bf16[7168,1536]{1,0:T(8,128)(2,1)} %param.16), kind=kOutput, calls=%fused_computation.10 | convolution fusion | flops 704741376 | bytes 22675584 | tf_op jit(solution)/shard_map/dot_general | solution.py:41
  20.9 15.2 %convolution_convert_fusion = bf16[32,12288]{1,0:T(8,128)(2,1)S(1)} fusion(bf16[1536,12288]{1,0:T(8,128)(2,1)} %param.18, f32[32,1536]{1,0:T(8,128)S(1)} %get-tuple-element.19, f32[1536]{0:T(1024)S(1)} %convert_element_type.27, f32[32]{0:T(128)S(1)} %add_rsqrt_fusion.1), kind=kOutput, calls=%fused_computation | convolution fusion | flops 1208500224 | bytes 38738048 | tf_op jit(solution)/shard_map/dot_general | solution.py:43
  36.1 1.2 reshape.82
  37.3 0.1 slice.37
  37.4 0.1 slice_convert_fusion
  37.5 0.6 subtract_convert_fusion
  38.1 1.1 pad_maximum_fusion.qpe_ref
  39.2 4.8 %fusion.1 = bf16[64,32,512]{2,1,0:T(8,128)(2,1)S(1)} fusion(bf16[64,128,512]{2,1,0:T(8,128)(2,1)} %param.21, bf16[32,64,128]{2,1,0:T(8,128)(2,1)S(1)} %slice.37), kind=kOutput, calls=%fused_computation.7 | convolution fusion | flops 268435456 | bytes 11010048 | tf_op jit(solution)/shard_map/bhn,hnc->bhc/dot_general | solution.py:47
  44.0 2.5 %copy.40 = bf16[64,32,512]{2,0,1:T(8,128)(2,1)} copy(bf16[64,32,512]{2,1,0:T(8,128)(2,1)S(1)} %fusion.1) | data formatting | bytes 4194304 | tf_op jit(solution)/shard_map/bhn,hnc->bhc/dot_general | solution.py:47
  46.5 54.0 %attend.1 = (bf16[32,2048,512]{2,1,0:T(8,128)(2,1)}, bf16[32,64,2048]{2,1,0:T(8,128)(2,1)}, f32[8,33,8,512]{3,2,1,0:T(8,128)}) custom-call(s32[32]{0:T(128)} %len_ref.1, bf16[32,64,512]{2,1,0:T(8,128)(2,1)} %bitcast.15, bf16[32,64,64]{2,1,0:T(8,128)(2,1)} %pad_maximum_fusion.qpe_ref, bf16[32,1,512]{2,1,0:T(2,128)(2,1)} %copy.30.ckvn_ref, ...), custom_call_target="tpu_custom_call" | custom-call | tf_op jit(solution)/shard_map/attend/pallas_call | solution.py:157
  100.5 0.0 copy-start.1
  100.5 72.1 %finish.1 = bf16[32,7168]{1,0:T(8,128)(2,1)} custom-call(f32[8,33,8,512]{3,2,1,0:T(8,128)} %get-tuple-element.7.terms, bf16[64,128,512]{2,1,0:T(8,128)(2,1)} %w_uv.1, bf16[8192,7168]{1,0:T(8,128)(2,1)} %w_out.1), custom_call_target="tpu_custom_call" | custom-call | tf_op jit(solution)/shard_map/finish/pallas_call | solution.py:290
  172.6 1.8 %copy.42 = bf16[32,7168]{1,0:T(8,128)(2,1)} copy(bf16[32,7168]{1,0:T(8,128)(2,1)} %finish.1) | data formatting | bytes 917504
  (6 shorter events, 0.0 us)
Async XLA Ops:
  0.6 2.1 %copy-start = (bf16[32,7168]{1,0:T(8,128)(2,1)S(1)}, bf16[32,7168]{1,0:T(8,128)(2,1)}, u32[]{:S(2)}) copy-start(bf16[32,7168]{1,0:T(8,128)(2,1)} %param.12) | copy-start | bytes 1376260
  100.5 73.9 %copy-start.1 = (bf16[32,7168]{1,0:T(8,128)(2,1)S(1)}, bf16[32,7168]{1,0:T(8,128)(2,1)}, u32[]{:S(2)}) copy-start(bf16[32,7168]{1,0:T(8,128)(2,1)} %param.12) | copy-start | bytes 1376260

commit v2 on v1

v2 whole, which is shorter than its diff:
```python
import functools

import jax
import jax.numpy as jnp
from jax import lax
from jax.experimental import pallas as pl
from jax.experimental.pallas import tpu as pltpu
from jax.sharding import PartitionSpec as P

EPS = 1e-6
ROPE_THETA = 10000.0
NEG_FILL = -1e30
MESH = pl.DeviceIdType.MESH
VMEM = pl.BlockSpec(memory_space=pltpu.VMEM)
SMEM = pl.BlockSpec(memory_space=pltpu.SMEM)
ANY = pl.BlockSpec(memory_space=pl.ANY)


def rope_tables(cache_len, rope_dim):
    inv_freq = jnp.power(ROPE_THETA, -2.0 * jnp.arange(rope_dim // 2, dtype=jnp.float32) / rope_dim)
    rope_angle = cache_len.astype(jnp.float32)[:, None] * inv_freq[None, :]
    return jnp.cos(rope_angle), jnp.sin(rope_angle)


def project_kernel(cfg, hidden, w_dq, w_dkv_t, w_uq, w_uk, q_gain, kv_gain, cos_t, sin_t, q_out, kvn_out, kv_new_out,
                   dq, dkv, uq, uk, halves, q_mine, q_theirs, turn, dq_sem, dkv_sem, uq_sem, uk_sem, h_ss, h_rs, q_ss, q_rs):
    n_seqs = hidden.shape[0]
    n_k, k_rows, dq_cols = dq.shape
    n_blk, _, blk = uq.shape
    dkv_cols = dkv.shape[0]
    n_kt = cfg["n_kt"]
    k_tile = dkv.shape[1] // n_kt
    lat_dim = cfg["lat_dim"]
    nope_dim = uk.shape[1]
    heads = uk.shape[0]
    half_heads = heads // 2
    group = cfg["group"]
    me = lax.axis_index('sp')
    c = me % 2
    partner = me - c + (1 - c)
    f32 = jnp.float32

    def load_dq(k):
        return pltpu.make_async_copy(w_dq.at[pl.ds(k * k_rows, k_rows), pl.ds(pl.multiple_of(c * dq_cols, 128), dq_cols)], dq.at[k], dq_sem.at[k])

    def load_dkv(k):
        return pltpu.make_async_copy(w_dkv_t.at[pl.ds(pl.multiple_of(c * (lat_dim // 2), 16), dkv_cols), pl.ds(k * k_tile, k_tile)], dkv.at[:, pl.ds(k * k_tile, k_tile)], dkv_sem.at[k])

    def load_uq(k):
        return pltpu.make_async_copy(w_uq.at[:, pl.ds(pl.multiple_of((c * n_blk + k) * blk, 128), blk)], uq.at[k], uq_sem.at[k])

    def load_uk(k):
        first = (c * half_heads + k * group) % heads
        return pltpu.make_async_copy(w_uk.at[pl.ds(first, group)], uk.at[pl.ds(k * group, group)], uk_sem.at[k])

    n_grp = heads // group
    per_kt = n_k // n_kt
    for k in range(n_k):
        load_dq(k).start()
        if k % per_kt == 0:
            load_dkv(k // per_kt).start()
    per_grp = n_blk // (n_grp // 2)
    for g in range(n_grp // 2):
        for k in range(per_grp):
            load_uq(g * per_grp + k).start()
        load_uk(g).start()
    for g in range(n_grp // 2, n_grp):
        load_uk(g).start()

    barrier = pltpu.get_barrier_semaphore()
    pl.semaphore_signal(barrier, inc=1, device_id={'sp': partner}, device_id_type=MESH)
    pl.semaphore_wait(barrier, 1)

    acc_q = jnp.zeros((n_seqs, dq_cols), f32)
    acc_kv = jnp.zeros((n_seqs, dkv_cols), f32)
    for k in range(n_k):
        load_dq(k).wait()
        acc_q = acc_q + jnp.dot(hidden[:, k * k_rows:(k + 1) * k_rows], dq[k], preferred_element_type=f32)
        if k % per_kt == per_kt - 1:
            t = k // per_kt
            load_dkv(t).wait()
            cols = slice(t * k_tile, (t + 1) * k_tile)
            acc_kv = acc_kv + lax.dot_general(hidden[:, cols], dkv[:, cols], (((1,), (1,)), ((), ())), preferred_element_type=f32)
    halves[c, :, dq_cols + lat_dim // 2:] = jnp.zeros((n_seqs, 128), f32)
    halves[c, :, :dq_cols] = acc_q
    halves[c, :, dq_cols:dq_cols + dkv_cols] = acc_kv
    swap = pltpu.make_async_remote_copy(src_ref=halves.at[c], dst_ref=halves.at[c], send_sem=h_ss, recv_sem=h_rs, device_id={'sp': partner}, device_id_type=MESH)
    swap.start()
    swap.wait_recv()

    lo, hi = halves[0], halves[1]
    raw_q = [lo[:, :dq_cols], hi[:, :dq_cols]]
    mean_sq = sum(jnp.sum(r * r, axis=1, keepdims=True) for r in raw_q) / (2 * dq_cols)
    inv = lax.rsqrt(mean_sq + EPS)
    c_q = jnp.concatenate([r * inv * q_gain[:, i * dq_cols:(i + 1) * dq_cols].astype(f32) for i, r in enumerate(raw_q)], axis=1).astype(jnp.bfloat16)

    lane = lax.broadcasted_iota(jnp.int32, (n_seqs, 128), 1)

    def rotate_pair(pair):
        other = jnp.where(lane % 64 < 32, pltpu.roll(pair, 96, 1), pltpu.roll(pair, 32, 1))
        return pair * cos_t[...] + other * sin_t[...]

    def emit(q_blk, k, at):
        for p in range(blk // 384):
            t0, t1, t2 = (q_blk[:, p * 384 + i * 128:p * 384 + (i + 1) * 128] for i in range(3))
            odd = jnp.where(lane < 64, pltpu.roll(t1, 64, 1), pltpu.roll(t2, 64, 1))
            pe = rotate_pair(jnp.where(lane < 64, t1, t2))
            for i, (nope, rope) in enumerate(((t0, pe), (odd, pltpu.roll(pe, 64, 1)))):
                h = k * (blk // 192) + p * 2 + i
                lat = jnp.dot(nope.astype(jnp.bfloat16), uk[at + h], preferred_element_type=f32)
                row = (h % group) * n_seqs
                for j in range(lat_dim // 128):
                    turn[j, row:row + n_seqs, :] = lat[:, j * 128:(j + 1) * 128]
                turn[lat_dim // 128, row:row + n_seqs, :] = rope

    def flush(first):
        rows = pl.ds(pl.multiple_of(first, group), group)
        for b in range(n_seqs):
            for j in range(lat_dim // 128 + 1):
                q_out[b, rows, j * 128:(j + 1) * 128] = turn[j, pl.ds(b, group, stride=n_seqs), :].astype(q_out.dtype)

    sends = []
    for k in range(n_blk):
        load_uq(k).wait()
        q_blk = jnp.dot(c_q, uq[k], preferred_element_type=f32).astype(jnp.bfloat16).astype(f32)
        q_mine[k] = q_blk
        sends.append(pltpu.make_async_remote_copy(src_ref=q_mine.at[k], dst_ref=q_theirs.at[k], send_sem=q_ss.at[k], recv_sem=q_rs.at[k], device_id={'sp': partner}, device_id_type=MESH))
        if k % per_grp == 0:
            load_uk(k // per_grp).wait()
        emit(q_blk, k, 0)
        sends[k].start()
        if k % per_grp == per_grp - 1:
            flush(c * half_heads + (k // per_grp) * group)

    raw_kv = [lo[:, dq_cols:dq_cols + lat_dim // 2], hi[:, dq_cols:dq_cols + lat_dim // 2]]
    mean_sq = sum(jnp.sum(r * r, axis=1, keepdims=True) for r in raw_kv) / lat_dim
    inv = lax.rsqrt(mean_sq + EPS)
    c_kv = jnp.concatenate([r * inv * kv_gain[:, i * (lat_dim // 2):(i + 1) * (lat_dim // 2)].astype(f32) for i, r in enumerate(raw_kv)], axis=1).astype(jnp.bfloat16)
    k_pe = rotate_pair(hi[:, dq_cols + lat_dim // 2:]).astype(jnp.bfloat16)
    kvn_out[:, :lat_dim] = c_kv.astype(f32)
    kvn_out[:, lat_dim:] = k_pe.astype(f32)
    kv_new_out[:, :lat_dim] = c_kv
    kv_new_out[:, lat_dim:] = k_pe[:, :64]

    for k in range(n_blk):
        sends[k].wait_recv()
        if k % per_grp == 0:
            load_uk(n_grp // 2 + k // per_grp).wait()
        emit(q_theirs[k], k, half_heads)
        if k % per_grp == per_grp - 1:
            flush((1 - c) * half_heads + (k // per_grp) * group)
    swap.wait_send()
    for s in sends:
        s.wait_send()


def project(hidden, cache_len, w_dq, q_gain, w_uq, w_dkv, kv_gain, w_uk):
    n_seqs, d_model = hidden.shape
    heads, nope_dim, lat_dim = w_uk.shape
    q_rank = w_dq.shape[1]
    rope_dim = w_dkv.shape[1] - lat_dim
    cos_t, sin_t = rope_tables(cache_len, rope_dim)
    cos_t = jnp.concatenate([cos_t] * 4, axis=1)
    sin_t = jnp.concatenate([-sin_t, sin_t] * 2, axis=1)
    cfg = dict(n_kt=4, lat_dim=lat_dim, group=16)
    n_k, n_blk = 8, 8
    dq_cols, dkv_cols = q_rank // 2, lat_dim // 2 + rope_dim
    blk = w_uq.shape[1] // 2 // n_blk
    f32, bf16 = jnp.float32, jnp.bfloat16
    dma = pltpu.SemaphoreType.DMA
    return pl.pallas_call(
        functools.partial(project_kernel, cfg),
        out_shape=(
            jax.ShapeDtypeStruct((n_seqs, heads, lat_dim + 128), bf16),
            jax.ShapeDtypeStruct((n_seqs, lat_dim + 128), f32),
            jax.ShapeDtypeStruct((n_seqs, lat_dim + rope_dim), bf16),
        ),
        in_specs=[VMEM, ANY, ANY, ANY, ANY, VMEM, VMEM, VMEM, VMEM],
        out_specs=(VMEM, VMEM, VMEM),
        scratch_shapes=[
            pltpu.VMEM((n_k, d_model // n_k, dq_cols), bf16),
            pltpu.VMEM((dkv_cols, d_model), bf16),
            pltpu.VMEM((n_blk, q_rank, blk), bf16),
            pltpu.VMEM((heads, nope_dim, lat_dim), bf16),
            pltpu.VMEM((2, n_seqs, dq_cols + lat_dim // 2 + 128), f32),
            pltpu.VMEM((n_blk, n_seqs, blk), f32),
            pltpu.VMEM((n_blk, n_seqs, blk), f32),
            pltpu.VMEM((lat_dim // 128 + 1, cfg["group"] * n_seqs, 128), f32),
            dma((n_k,)), dma((cfg["n_kt"],)), dma((n_blk,)), dma((heads // cfg["group"],)),
            dma, dma, dma((n_blk,)), dma((n_blk,)),
        ],
        compiler_params=pltpu.CompilerParams(collective_id=1, has_side_effects=True, vmem_limit_bytes=56 * 1024 * 1024),
        name="project",
    )(hidden, w_dq, w_dkv.T, w_uq, w_uk, q_gain.reshape(1, -1), kv_gain.reshape(1, -1), cos_t, sin_t)


def attend_kernel(cfg, len_ref, q_ref, kvn_ref, ckv_hbm, kpe_hbm, cout_hbm, kout_hbm, o_hbm,
                  cbuf, kbuf, obuf, peaks, denoms, isem, osem, psem):
    n_seqs, shard_len = ckv_hbm.shape[0], ckv_hbm.shape[1]
    lat_dim = ckv_hbm.shape[2]
    rope_dim = kpe_hbm.shape[1]
    per = o_hbm.shape[2] - 1
    n_buf, lag, chunk = cfg["n_buf"], cfg["lag"], cfg["chunk"]
    base = lax.axis_index('sp') * shard_len

    def copies_in(b, slot):
        return (pltpu.make_async_copy(ckv_hbm.at[b], cbuf.at[slot], isem.at[slot, 0]),
                pltpu.make_async_copy(kpe_hbm.at[b], kbuf.at[slot], isem.at[slot, 1]))

    def copies_out(b, slot):
        return (pltpu.make_async_copy(cbuf.at[slot], cout_hbm.at[b], osem.at[slot, 0]),
                pltpu.make_async_copy(kbuf.at[slot], kout_hbm.at[b], osem.at[slot, 1]))

    def copy_terms(b, side):
        return pltpu.make_async_copy(obuf.at[side], o_hbm.at[:, b // per, b % per], psem.at[side])

    def copy_stats(part):
        return pltpu.make_async_copy(obuf.at[0], o_hbm.at[:, part, per], psem.at[part])

    for i in range(n_buf - lag):
        for c in copies_in(i, i):
            c.start()
    peaks[...] = jnp.zeros_like(peaks)
    denoms[...] = jnp.zeros_like(denoms)

    def step(b, carry):
        slot = lax.rem(b, n_buf)

        @pl.when(b >= lag)
        def _():
            for c in copies_out(b - lag, lax.rem(b - lag + n_buf, n_buf)):
                c.wait()

        ahead = b - lag + n_buf

        @pl.when(ahead < n_seqs)
        def _():
            for c in copies_in(ahead, lax.rem(ahead, n_buf)):
                c.start()

        for c in copies_in(b, slot):
            c.wait()
        last = len_ref[b] - base

        @pl.when((last >= 0) & (last < shard_len))
        def _():
            picked = lax.broadcasted_iota(jnp.int32, kvn_ref.shape, 0) == b
            fresh_row = jnp.sum(jnp.where(picked, kvn_ref[...], 0.0), axis=0, keepdims=True)
            r0 = pl.multiple_of((last // 16) * 16, 16)
            rows = cbuf[slot, pl.ds(r0, 16), :].astype(jnp.float32)
            row = lax.broadcasted_iota(jnp.int32, rows.shape, 0)
            cbuf[slot, pl.ds(r0, 16), :] = jnp.where(row == last - r0, fresh_row[:, :lat_dim], rows).astype(cbuf.dtype)
            c0 = pl.multiple_of((last // 128) * 128, 128)
            cols = kbuf[slot, :, pl.ds(c0, 128)].astype(jnp.float32)
            lane = lax.broadcasted_iota(jnp.int32, cols.shape, 1)
            diag = lane == lax.broadcasted_iota(jnp.int32, cols.shape, 0)
            fresh = jnp.sum(jnp.where(diag, fresh_row[:, lat_dim:], 0.0), axis=1, keepdims=True)
            kbuf[slot, :, pl.ds(c0, 128)] = jnp.where(lane == last - c0, fresh, cols).astype(kbuf.dtype)

        q_lat, q_pe = q_ref[b, :, :lat_dim], q_ref[b, :, lat_dim:lat_dim + rope_dim]
        scores = []
        for t in range(0, shard_len, chunk):
            s = lax.dot_general(q_lat, cbuf[slot, t:t + chunk, :], (((1,), (1,)), ((), ())), preferred_element_type=jnp.float32)
            s = s + jnp.dot(q_pe, kbuf[slot, :, t:t + chunk], preferred_element_type=jnp.float32)
            pos = lax.broadcasted_iota(jnp.int32, (1, chunk), 1) + t
            scores.append(jnp.where(pos <= last, s * cfg["scale"], NEG_FILL))
        peak = functools.reduce(jnp.maximum, [jnp.max(s, axis=1, keepdims=True) for s in scores])
        denom = jnp.zeros_like(peak)
        lat_sum = None
        for k, t in enumerate(range(0, shard_len, chunk)):
            w = jnp.exp(scores[k] - peak)
            denom = denom + jnp.sum(w, axis=1, keepdims=True)
            term = jnp.dot(w.astype(jnp.bfloat16), cbuf[slot, t:t + chunk, :], preferred_element_type=jnp.float32)
            lat_sum = term if lat_sum is None else lat_sum + term
        for c in copies_out(b, slot):
            c.start()
        side = lax.rem(b, 2)

        @pl.when(b >= 2)
        def _():
            copy_terms(b - 2, side).wait()

        obuf[side] = lat_sum.reshape(obuf.shape[1:])
        lane = lax.broadcasted_iota(jnp.int32, peaks.shape, 1)
        peaks[...] = jnp.where(lane == b, peak, peaks[...])
        denoms[...] = jnp.where(lane == b, denom, denoms[...])
        copy_terms(b, side).start()
        return carry

    lax.fori_loop(0, n_seqs, step, 0)
    for i in range(n_seqs - 2, n_seqs):
        copy_terms(i, i % 2).wait()
    obuf[0, :, :, 0:128] = peaks[...].reshape(obuf.shape[1], obuf.shape[2], 128)
    obuf[0, :, :, 128:256] = denoms[...].reshape(obuf.shape[1], obuf.shape[2], 128)
    for i in range(n_seqs - lag, n_seqs):
        for c in copies_out(i, i % n_buf):
            c.wait()
    for part in range(2):
        copy_stats(part).start()
    for part in range(2):
        copy_stats(part).wait()


def attend(q, kvn, cache_len, ckv_blk, kpe_blk_t, n_dev, qk_dim):
    n_seqs, shard_len, lat_dim = ckv_blk.shape
    rope_dim = kpe_blk_t.shape[1]
    n_heads = q.shape[1]
    cfg = dict(n_buf=8, lag=3, chunk=512, scale=qk_dim ** -0.5)
    terms_shape = (n_dev, 2, n_seqs // 2 + 1, n_heads // n_dev, lat_dim)
    return pl.pallas_call(
        functools.partial(attend_kernel, cfg),
        out_shape=(
            jax.ShapeDtypeStruct(ckv_blk.shape, ckv_blk.dtype),
            jax.ShapeDtypeStruct(kpe_blk_t.shape, kpe_blk_t.dtype),
            jax.ShapeDtypeStruct(terms_shape, jnp.float32),
        ),
        in_specs=[SMEM, VMEM, VMEM, ANY, ANY],
        out_specs=(ANY, ANY, ANY),
        scratch_shapes=[
            pltpu.VMEM((cfg["n_buf"], shard_len, lat_dim), ckv_blk.dtype),
            pltpu.VMEM((cfg["n_buf"], rope_dim, shard_len), kpe_blk_t.dtype),
            pltpu.VMEM((2, n_dev, n_heads // n_dev, lat_dim), jnp.float32),
            pltpu.VMEM((n_heads, 128), jnp.float32),
            pltpu.VMEM((n_heads, 128), jnp.float32),
            pltpu.SemaphoreType.DMA((cfg["n_buf"], 2)),
            pltpu.SemaphoreType.DMA((cfg["n_buf"], 2)),
            pltpu.SemaphoreType.DMA((2,)),
        ],
        compiler_params=pltpu.CompilerParams(vmem_limit_bytes=56 * 1024 * 1024),
        name="attend",
    )(cache_len, q, kvn, ckv_blk, kpe_blk_t)


def finish_kernel(terms, w_uv, w_out, out_ref, own, pair, from_x, from_y, uv, wo, merged, oheads, psend, precv, isend, irecv, fin, agr, agp,
                  lsem, own_sem, d_ss, d_rs, x_ss, x_rs, y_ss, y_rs, p_ss, p_rs, i_ss, i_rs, a_ss, a_rs, f_ss, f_rs):
    n_seqs, width = fin.shape
    heads = uv.shape[0]
    depth = wo.shape[0]
    me = lax.axis_index('sp')
    y, x, c = me // 4, (me // 2) % 2, me % 2

    def device(q, jc):
        return ((y + q // 2) % 2) * 4 + ((x + q % 2) % 2) * 2 + (c + jc) % 2

    def send(src, dst, ss, rs, dev):
        return pltpu.make_async_remote_copy(src_ref=src, dst_ref=dst, send_sem=ss, recv_sem=rs, device_id={'sp': dev}, device_id_type=MESH)

    load_uv = pltpu.make_async_copy(w_uv.at[pl.ds(me * heads, heads)], uv, lsem.at[0])
    load_wo = pltpu.make_async_copy(w_out.at[pl.ds(me * depth, depth)], wo, lsem.at[1])
    order = ((3, 0), (3, 1), (1, 0), (2, 1), (2, 0), (1, 1), (0, 0), (0, 1))
    per = n_seqs // 2
    loads = {(q, h): pltpu.make_async_copy(terms.at[device(q, 0), h], own.at[q, h], own_sem.at[q, h]) for q, h in order}
    for k in order:
        loads[k].start()
    load_uv.start()
    load_wo.start()

    others = ((0, 1), (1, 0), (2, 0), (3, 0))
    barrier = pltpu.get_barrier_semaphore()
    for q, jc in others:
        pl.semaphore_signal(barrier, inc=1, device_id={'sp': device(q, jc)}, device_id_type=MESH)
    pl.semaphore_wait(barrier, len(others))

    d_sends = {(q, h): send(terms.at[device(q, 1), h], pair.at[q, h], d_ss.at[q, h], d_rs.at[q, h], device(0, 1)) for q, h in order}
    for k in order:
        d_sends[k].start()

    def merge(dst, src, h):
        old, new = dst[per, :, :128], src[per, :, :128]
        peak = jnp.maximum(old, new)
        f_old, f_new = jnp.exp(old - peak), jnp.exp(new - peak)
        dst[per, :, :128] = peak
        dst[per, :, 128:256] = f_old * dst[per, :, 128:256] + f_new * src[per, :, 128:256]
        for i in range(per):
            b = h * per + i
            dst[i] = f_old[:, b:b + 1] * dst[i] + f_new[:, b:b + 1] * src[i]

    def merge_pair(q, h):
        loads[q, h].wait()
        d_sends[q, h].wait_recv()
        merge(own.at[q, h], pair.at[q, h], h)

    x_dev, y_dev = device(1, 0), device(2, 0)
    x_sends = [send(own.at[k], from_x.at[i], x_ss.at[i], x_rs.at[i], x_dev) for i, k in enumerate(((3, 0), (1, 0), (1, 1)))]
    y_sends = [send(own.at[k], from_y.at[i], y_ss.at[i], y_rs.at[i], y_dev) for i, k in enumerate(((3, 1), (2, 1), (2, 0)))]
    merge_pair(3, 0)
    merge_pair(3, 1)
    x_sends[0].start()
    merge_pair(1, 0)
    y_sends[0].start()
    merge_pair(2, 1)
    x_sends[1].start()
    merge_pair(2, 0)
    y_sends[1].start()
    merge_pair(1, 1)
    merge_pair(0, 0)
    merge_pair(0, 1)
    x_sends[0].wait_recv()
    merge(own.at[2, 0], from_x.at[0], 0)
    y_sends[0].wait_recv()
    merge(own.at[1, 1], from_y.at[0], 1)
    y_sends[2].start()
    x_sends[2].start()
    x_sends[1].wait_recv()
    merge(own.at[0, 0], from_x.at[1], 0)
    y_sends[1].wait_recv()
    merge(own.at[0, 1], from_y.at[1], 1)
    y_sends[2].wait_recv()
    merge(own.at[0, 0], from_y.at[2], 0)
    x_sends[2].wait_recv()
    merge(own.at[0, 1], from_x.at[2], 1)
    for h in range(2):
        inv = 1.0 / own[0, h, per, :, 128:256]
        for i in range(per):
            b = h * per + i
            acc = inv[:, b:b + 1] * own[0, h, i]
            for k in range(merged.shape[0]):
                merged[k, b * heads:(b + 1) * heads, :] = acc[:, k * 128:(k + 1) * 128]
    load_uv.wait()
    for h in range(heads):
        o_lat = jnp.concatenate([merged[k, pl.ds(h, n_seqs, stride=heads), :] for k in range(merged.shape[0])], axis=1).astype(jnp.bfloat16)
        o_h = lax.dot_general(o_lat, uv[h], (((1,), (1,)), ((), ())), preferred_element_type=jnp.float32)
        oheads[:, h * o_h.shape[1]:(h + 1) * o_h.shape[1]] = o_h.astype(jnp.bfloat16)
    load_wo.wait()

    def partial_out(dev):
        cols = pl.ds(pl.multiple_of(dev * width, 128), width)
        return jnp.dot(oheads[...], wo[:, cols], preferred_element_type=jnp.float32)

    waiting = []
    p_sends, i_sends = {}, []
    for q in (3, 1, 2, 0):
        psend[q] = partial_out(device(q, 1))
        p_sends[q] = send(psend.at[q], precv.at[q], p_ss.at[q], p_rs.at[q], device(0, 1))
        for w in waiting:
            w.start()
        waiting = [p_sends[q]]
    mine = None
    for q in (3, 1, 2, 0):
        part = partial_out(device(q, 0))
        for w in waiting:
            w.start()
        waiting = []
        p_sends[q].wait_recv()
        if q:
            isend[q - 1] = part + precv[q]
            i_sends.append(send(isend.at[q - 1], irecv.at[q - 1], i_ss.at[q - 1], i_rs.at[q - 1], device(q, 0)))
            waiting = [i_sends[-1]]
        else:
            mine = part + precv[0]
    for s in i_sends:
        s.wait_recv()
    result = mine + irecv[0] + irecv[1] + irecv[2]
    fin[...] = result
    out_ref[:, pl.ds(pl.multiple_of(me * width, 128), width)] = result.astype(out_ref.dtype)

    a_sends = {q: send(fin, agr.at[q - 1], a_ss.at[q - 1], a_rs.at[q - 1], device(q, 0)) for q in (3, 1, 2)}
    f_sends = {0: send(fin, agp.at[0], f_ss.at[0], f_rs.at[0], device(0, 1))}
    for q in (3, 1, 2):
        a_sends[q].start()
    f_sends[0].start()
    for q in (1, 2, 3):
        f_sends[q] = send(agr.at[q - 1], agp.at[q], f_ss.at[q], f_rs.at[q], device(0, 1))
        a_sends[q].wait_recv()
        f_sends[q].start()
        out_ref[:, pl.ds(pl.multiple_of(device(q, 0) * width, 128), width)] = agr[q - 1].astype(out_ref.dtype)
    for q in range(4):
        f_sends[q].wait_recv()
        out_ref[:, pl.ds(pl.multiple_of(device(q, 1) * width, 128), width)] = agp[q].astype(out_ref.dtype)
    for s in list(d_sends.values()) + x_sends + y_sends + list(p_sends.values()) + i_sends + list(a_sends.values()) + list(f_sends.values()):
        s.wait_send()


def finish(terms, w_uv, w_out):
    n_dev, _, rows, heads, lat_dim = terms.shape
    n_seqs = 2 * (rows - 1)
    d_model = w_out.shape[1]
    depth = w_out.shape[0] // n_dev
    width = d_model // n_dev
    f32 = jnp.float32
    return pl.pallas_call(
        finish_kernel,
        out_shape=jax.ShapeDtypeStruct((n_seqs, d_model), jnp.bfloat16),
        in_specs=[ANY, ANY, ANY],
        out_specs=VMEM,
        scratch_shapes=[
            pltpu.VMEM((4, 2, rows, heads, lat_dim), f32),
            pltpu.VMEM((4, 2, rows, heads, lat_dim), f32),
            pltpu.VMEM((3, rows, heads, lat_dim), f32),
            pltpu.VMEM((3, rows, heads, lat_dim), f32),
            pltpu.VMEM((heads,) + w_uv.shape[1:], w_uv.dtype),
            pltpu.VMEM((depth, d_model), w_out.dtype),
            pltpu.VMEM((lat_dim // 128, n_seqs * heads, 128), f32),
            pltpu.VMEM((n_seqs, depth), jnp.bfloat16),
            pltpu.VMEM((4, n_seqs, width), f32),
            pltpu.VMEM((4, n_seqs, width), f32),
            pltpu.VMEM((3, n_seqs, width), f32),
            pltpu.VMEM((3, n_seqs, width), f32),
            pltpu.VMEM((n_seqs, width), f32),
            pltpu.VMEM((3, n_seqs, width), f32),
            pltpu.VMEM((4, n_seqs, width), f32),
            pltpu.SemaphoreType.DMA((2,)),
            pltpu.SemaphoreType.DMA((4, 2)),
            pltpu.SemaphoreType.DMA((4, 2)),
            pltpu.SemaphoreType.DMA((4, 2)),
            pltpu.SemaphoreType.DMA((3,)),
            pltpu.SemaphoreType.DMA((3,)),
            pltpu.SemaphoreType.DMA((3,)),
            pltpu.SemaphoreType.DMA((3,)),
            pltpu.SemaphoreType.DMA((4,)),
            pltpu.SemaphoreType.DMA((4,)),
            pltpu.SemaphoreType.DMA((3,)),
            pltpu.SemaphoreType.DMA((3,)),
            pltpu.SemaphoreType.DMA((3,)),
            pltpu.SemaphoreType.DMA((3,)),
            pltpu.SemaphoreType.DMA((4,)),
            pltpu.SemaphoreType.DMA((4,)),
        ],
        compiler_params=pltpu.CompilerParams(collective_id=0, has_side_effects=True, vmem_limit_bytes=56 * 1024 * 1024),
        name="finish",
    )(terms, w_uv, w_out)


def solution(mesh):
    n_dev = mesh.shape['sp']

    def local_step(hidden, ckv_blk, kpe_blk, cache_len, w_dq, q_gain, w_uq, w_dkv, kv_gain, w_uk, w_uv, w_out):
        q, kvn, kv_new = project(hidden, cache_len, w_dq, q_gain, w_uq, w_dkv, kv_gain, w_uk)
        qk_dim = w_uk.shape[1] + kpe_blk.shape[2]
        ckv_out, kpe_out_t, terms = attend(q, kvn, cache_len, ckv_blk, jnp.swapaxes(kpe_blk, 1, 2), n_dev, qk_dim)
        out = finish(terms, w_uv, w_out)
        return out, ckv_out, jnp.swapaxes(kpe_out_t, 1, 2), kv_new

    cache_spec = P('dp', 'sp', None)
    return jax.shard_map(local_step, mesh=mesh, in_specs=(P('dp', None), cache_spec, cache_spec, P('dp'), P(), P(), P(), P(), P(), P(), P(), P()), out_specs=(P('dp', None), cache_spec, cache_spec, P('dp', None)), check_vma=False)
```

time: 175 us -> 137 us (0.78)
  matrix products: 35.1 us -> 0 us
  Pallas kernels: 126 us -> 130 us
  other arithmetic: 5.07 us -> 1.52 us
  local copies, waits for them, and re-layouts: 7.41 us -> 4.98 us
    dot_general x4 -> x0, matrix products: 35.1 us -> none  [the longest x1 15.2 us: project_token(): jnp.dot(c_q, w_uq, preferred_element_type=jnp.float32).astype(jnp.bfloat16)]
    pallas_call x0 -> x1, Pallas kernels: none -> 30.2 us  [project(): pl.pallas_call(functools.partial(project_kernel, cfg), out_shape=(jax.Sha...]
    pallas_call x1, Pallas kernels: 72.1 us -> 45.5 us  [finish(): pl.pallas_call(finish_kernel, out_shape=jax.ShapeDtypeStruct((n_seqs, d_m...]
    dot_general x1 -> x0, local copies, waits for them, and re-layouts: 2.48 us -> none  [project_token(): jnp.einsum('bhn,hnc->bhc', q_full[:, :, :nope_dim], w_uk, preferred_eleme...]
where the time goes in v2:
time: 137 us
  Pallas kernels  130 us (95%)
  local copies, waits for them, and re-layouts  4.98 us (4%)
  other arithmetic  1.52 us (1%)
    pallas_call x1, Pallas kernels, attend(): pl.pallas_call(functools.partial(attend_kernel, cfg), out_shape=(jax.Shap...  53.9 us
    pallas_call x1, Pallas kernels, finish(): pl.pallas_call(finish_kernel, out_shape=jax.ShapeDtypeStruct((n_seqs, d_m...  45.5 us
    pallas_call x1, Pallas kernels, project(): pl.pallas_call(functools.partial(project_kernel, cfg), out_shape=(jax.Sha...  30.2 us

profile of v2, /device:TPU:0, one launch (start us, length us, event | category | flops | bytes accessed | tf_op | source)
XLA Modules:
  0.0 136.7 jit_solution(8355357869021706992)
XLA Ops:
  0.6 0.7 convert_element_type.3
  1.3 1.3 reshape.21.kv_gain
  2.6 1.3 reshape.20.q_gain
  3.8 0.1 fusion
  4.0 0.7 pad_maximum_fusion
  4.7 30.2 %project.1 = (bf16[32,64,640]{2,1,0:T(8,128)(2,1)}, f32[32,640]{1,0:T(8,128)}, bf16[32,576]{1,0:T(8,128)(2,1)}) custom-call(bf16[32,7168]{1,0:T(8,128)(2,1)} %hidden.1, bf16[7168,1536]{1,0:T(8,128)(2,1)} %w_dq.1, bf16[576,7168]{1,0:T(8,128)(2,1)} %bitcast.4, bf16[1536,12288]{1,0:T(8,128)(2,1)} %w_uq.1, bf16[64,128,512]{2,1,0:T(8,128)(2,1)} %w_uk.1, ...), custom_call_target="tpu_custom_call" | custom-call | tf_op jit(solution)/shard_map/project/pallas_call | solution.py:171
  34.9 53.9 %attend.1 = (bf16[32,2048,512]{2,1,0:T(8,128)(2,1)}, bf16[32,64,2048]{2,1,0:T(8,128)(2,1)}, f32[8,2,17,8,512]{4,3,2,1,0:T(8,128)}) custom-call(s32[32]{0:T(128)} %len_ref.1, bf16[32,64,640]{2,1,0:T(8,128)(2,1)} %get-tuple-element.10.q_ref, f32[32,640]{1,0:T(8,128)} %get-tuple-element.11.kvn_ref, bf16[32,2048,512]{2,1,0:T(8,128)(2,1)} %ckv_hbm.1, ...), custom_call_target="tpu_custom_call" | custom-call | tf_op jit(solution)/shard_map/attend/pallas_call | solution.py:310
  88.8 0.0 copy-start
  88.8 45.5 %finish.1 = bf16[32,7168]{1,0:T(8,128)(2,1)} custom-call(f32[8,2,17,8,512]{4,3,2,1,0:T(8,128)} %get-tuple-element.12.terms, bf16[64,128,512]{2,1,0:T(8,128)(2,1)} %w_uv.1, bf16[8192,7168]{1,0:T(8,128)(2,1)} %w_out.1), custom_call_target="tpu_custom_call" | custom-call | tf_op jit(solution)/shard_map/finish/pallas_call | solution.py:481
  134.3 1.8 %copy.18 = bf16[32,7168]{1,0:T(8,128)(2,1)} copy(bf16[32,7168]{1,0:T(8,128)(2,1)} %finish.1) | data formatting | bytes 917504
  136.1 0.0 copy-done
  136.1 0.6 copy.19
  (1 shorter events, 0.0 us)
Async XLA Ops:
  88.8 47.3 %copy-start = (bf16[32,576]{1,0:T(8,128)(2,1)S(1)}, bf16[32,576]{1,0:T(8,128)(2,1)}, u32[]{:S(2)}) copy-start(bf16[32,576]{1,0:T(8,128)(2,1)} %get-tuple-element.28) | copy-start | bytes 110596

commit v3 on v2

--- a/solution.py
+++ b/solution.py
@@ -2,6 +2,7 @@
 
 import jax
 import jax.numpy as jnp
+import numpy as np
 from jax import lax
 from jax.experimental import pallas as pl
 from jax.experimental.pallas import tpu as pltpu
@@ -16,13 +17,7 @@
 ANY = pl.BlockSpec(memory_space=pl.ANY)
 
 
-def rope_tables(cache_len, rope_dim):
-    inv_freq = jnp.power(ROPE_THETA, -2.0 * jnp.arange(rope_dim // 2, dtype=jnp.float32) / rope_dim)
-    rope_angle = cache_len.astype(jnp.float32)[:, None] * inv_freq[None, :]
-    return jnp.cos(rope_angle), jnp.sin(rope_angle)
-
-
-def project_kernel(cfg, hidden, w_dq, w_dkv_t, w_uq, w_uk, q_gain, kv_gain, cos_t, sin_t, q_out, kvn_out, kv_new_out,
+def project_kernel(cfg, len_ref, hidden, w_dq, w_dkv_t, w_uq, w_uk, q_gain_ref, kv_gain_ref, freq, q_out, kvn_out,
                    dq, dkv, uq, uk, halves, q_mine, q_theirs, turn, dq_sem, dkv_sem, uq_sem, uk_sem, h_ss, h_rs, q_ss, q_rs):
     n_seqs = hidden.shape[0]
     n_k, k_rows, dq_cols = dq.shape
@@ -34,7 +29,7 @@
     nope_dim = uk.shape[1]
     heads = uk.shape[0]
     half_heads = heads // 2
-    group = cfg["group"]
+    group, pitch = cfg["group"], cfg["pitch"]
     me = lax.axis_index('sp')
     c = me % 2
     partner = me - c + (1 - c)
@@ -55,30 +50,51 @@
 
     n_grp = heads // group
     per_kt = n_k // n_kt
+    per_grp = n_blk // (n_grp // 2)
+    loads = []
     for k in range(n_k):
-        load_dq(k).start()
+        loads.append(load_dq(k))
         if k % per_kt == 0:
-            load_dkv(k // per_kt).start()
-    per_grp = n_blk // (n_grp // 2)
-    for g in range(n_grp // 2):
-        for k in range(per_grp):
-            load_uq(g * per_grp + k).start()
-        load_uk(g).start()
-    for g in range(n_grp // 2, n_grp):
-        load_uk(g).start()
+            loads.append(load_dkv(k // per_kt))
+    for k in range(n_blk):
+        loads.append(load_uq(k))
+        if k % per_grp == 0:
+            loads.append(load_uk(k // per_grp))
+        if k >= cfg["behind"] and (k - cfg["behind"]) % per_grp == 0:
+            loads.append(load_uk(n_grp // 2 + (k - cfg["behind"]) // per_grp))
+    in_flight = cfg["in_flight"]
+    for load in loads[:in_flight]:
+        load.start()
+    queue = loads[in_flight:]
+
+    def wait_load(load):
+        load.wait()
+        if queue:
+            queue.pop(0).start()
 
     barrier = pltpu.get_barrier_semaphore()
     pl.semaphore_signal(barrier, inc=1, device_id={'sp': partner}, device_id_type=MESH)
     pl.semaphore_wait(barrier, 1)
 
+    lane = lax.broadcasted_iota(jnp.int32, (n_seqs, 128), 1)
+    row = lax.broadcasted_iota(jnp.int32, (n_seqs, 128), 0)
+    position = jnp.zeros((n_seqs, 128), f32)
+    for b in range(n_seqs):
+        position = jnp.where(row == b, len_ref[b].astype(f32), position)
+    angle = position * freq[...]
+    cos_t = jnp.cos(angle)
+    sin_t = jnp.where(lane % 64 < 32, -jnp.sin(angle), jnp.sin(angle))
+    q_gain = q_gain_ref[...].astype(f32).reshape(1, -1)
+    kv_gain = kv_gain_ref[...].astype(f32).reshape(1, -1)
+
     acc_q = jnp.zeros((n_seqs, dq_cols), f32)
     acc_kv = jnp.zeros((n_seqs, dkv_cols), f32)
     for k in range(n_k):
-        load_dq(k).wait()
+        wait_load(load_dq(k))
         acc_q = acc_q + jnp.dot(hidden[:, k * k_rows:(k + 1) * k_rows], dq[k], preferred_element_type=f32)
         if k % per_kt == per_kt - 1:
             t = k // per_kt
-            load_dkv(t).wait()
+            wait_load(load_dkv(t))
             cols = slice(t * k_tile, (t + 1) * k_tile)
             acc_kv = acc_kv + lax.dot_general(hidden[:, cols], dkv[:, cols], (((1,), (1,)), ((), ())), preferred_element_type=f32)
     halves[c, :, dq_cols + lat_dim // 2:] = jnp.zeros((n_seqs, 128), f32)
@@ -92,63 +108,68 @@
     raw_q = [lo[:, :dq_cols], hi[:, :dq_cols]]
     mean_sq = sum(jnp.sum(r * r, axis=1, keepdims=True) for r in raw_q) / (2 * dq_cols)
     inv = lax.rsqrt(mean_sq + EPS)
-    c_q = jnp.concatenate([r * inv * q_gain[:, i * dq_cols:(i + 1) * dq_cols].astype(f32) for i, r in enumerate(raw_q)], axis=1).astype(jnp.bfloat16)
-
-    lane = lax.broadcasted_iota(jnp.int32, (n_seqs, 128), 1)
+    c_q = jnp.concatenate([r * inv * q_gain[:, i * dq_cols:(i + 1) * dq_cols] for i, r in enumerate(raw_q)], axis=1).astype(jnp.bfloat16)
 
     def rotate_pair(pair):
         other = jnp.where(lane % 64 < 32, pltpu.roll(pair, 96, 1), pltpu.roll(pair, 32, 1))
-        return pair * cos_t[...] + other * sin_t[...]
-
-    def emit(q_blk, k, at):
+        return pair * cos_t + other * sin_t
+
+    def emit(q_blk, k, side):
         for p in range(blk // 384):
             t0, t1, t2 = (q_blk[:, p * 384 + i * 128:p * 384 + (i + 1) * 128] for i in range(3))
             odd = jnp.where(lane < 64, pltpu.roll(t1, 64, 1), pltpu.roll(t2, 64, 1))
             pe = rotate_pair(jnp.where(lane < 64, t1, t2))
             for i, (nope, rope) in enumerate(((t0, pe), (odd, pltpu.roll(pe, 64, 1)))):
                 h = k * (blk // 192) + p * 2 + i
-                lat = jnp.dot(nope.astype(jnp.bfloat16), uk[at + h], preferred_element_type=f32)
-                row = (h % group) * n_seqs
+                lat = jnp.dot(nope.astype(jnp.bfloat16), uk[side * half_heads + h], preferred_element_type=f32)
+                first = (h % group) * pitch
                 for j in range(lat_dim // 128):
-                    turn[j, row:row + n_seqs, :] = lat[:, j * 128:(j + 1) * 128]
-                turn[lat_dim // 128, row:row + n_seqs, :] = rope
-
-    def flush(first):
+                    turn[side, j, first:first + n_seqs, :] = lat[:, j * 128:(j + 1) * 128]
+                turn[side, lat_dim // 128, first:first + n_seqs, :] = rope
+
+    def flush(first, side):
         rows = pl.ds(pl.multiple_of(first, group), group)
         for b in range(n_seqs):
             for j in range(lat_dim // 128 + 1):
-                q_out[b, rows, j * 128:(j + 1) * 128] = turn[j, pl.ds(b, group, stride=n_seqs), :].astype(q_out.dtype)
+                q_out[b, rows, j * 128:(j + 1) * 128] = turn[side, j, pl.ds(b, group, stride=pitch), :].astype(q_out.dtype)
 
     sends = []
-    for k in range(n_blk):
-        load_uq(k).wait()
+
+    def own_block(k):
+        wait_load(load_uq(k))
         q_blk = jnp.dot(c_q, uq[k], preferred_element_type=f32).astype(jnp.bfloat16).astype(f32)
         q_mine[k] = q_blk
         sends.append(pltpu.make_async_remote_copy(src_ref=q_mine.at[k], dst_ref=q_theirs.at[k], send_sem=q_ss.at[k], recv_sem=q_rs.at[k], device_id={'sp': partner}, device_id_type=MESH))
         if k % per_grp == 0:
-            load_uk(k // per_grp).wait()
+            wait_load(load_uk(k // per_grp))
         emit(q_blk, k, 0)
         sends[k].start()
         if k % per_grp == per_grp - 1:
-            flush(c * half_heads + (k // per_grp) * group)
-
+            flush(c * half_heads + (k // per_grp) * group, 0)
+
+    def their_block(k):
+        sends[k].wait_recv()
+        if k % per_grp == 0:
+            wait_load(load_uk(n_grp // 2 + k // per_grp))
+        emit(q_theirs[k], k, 1)
+        if k % per_grp == per_grp - 1:
+            flush((1 - c) * half_heads + (k // per_grp) * group, 1)
+
+    behind = cfg["behind"]
+    for k in range(n_blk):
+        own_block(k)
+        if k >= behind:
+            their_block(k - behind)
     raw_kv = [lo[:, dq_cols:dq_cols + lat_dim // 2], hi[:, dq_cols:dq_cols + lat_dim // 2]]
     mean_sq = sum(jnp.sum(r * r, axis=1, keepdims=True) for r in raw_kv) / lat_dim
     inv = lax.rsqrt(mean_sq + EPS)
-    c_kv = jnp.concatenate([r * inv * kv_gain[:, i * (lat_dim // 2):(i + 1) * (lat_dim // 2)].astype(f32) for i, r in enumerate(raw_kv)], axis=1).astype(jnp.bfloat16)
+    c_kv = jnp.concatenate([r * inv * kv_gain[:, i * (lat_dim // 2):(i + 1) * (lat_dim // 2)] for i, r in enumerate(raw_kv)], axis=1).astype(jnp.bfloat16)
     k_pe = rotate_pair(hi[:, dq_cols + lat_dim // 2:]).astype(jnp.bfloat16)
     kvn_out[:, :lat_dim] = c_kv.astype(f32)
     kvn_out[:, lat_dim:] = k_pe.astype(f32)
-    kv_new_out[:, :lat_dim] = c_kv
-    kv_new_out[:, lat_dim:] = k_pe[:, :64]
-
-    for k in range(n_blk):
-        sends[k].wait_recv()
-        if k % per_grp == 0:
-            load_uk(n_grp // 2 + k // per_grp).wait()
-        emit(q_theirs[k], k, half_heads)
-        if k % per_grp == per_grp - 1:
-            flush((1 - c) * half_heads + (k // per_grp) * group)
+
+    for k in range(n_blk - behind, n_blk):
+        their_block(k)
     swap.wait_send()
     for s in sends:
         s.wait_send()
@@ -159,10 +180,9 @@
     heads, nope_dim, lat_dim = w_uk.shape
     q_rank = w_dq.shape[1]
     rope_dim = w_dkv.shape[1] - lat_dim
-    cos_t, sin_t = rope_tables(cache_len, rope_dim)
-    cos_t = jnp.concatenate([cos_t] * 4, axis=1)
-    sin_t = jnp.concatenate([-sin_t, sin_t] * 2, axis=1)
-    cfg = dict(n_kt=4, lat_dim=lat_dim, group=16)
+    freq = np.power(ROPE_THETA, -2.0 * np.arange(rope_dim // 2) / rope_dim).astype(np.float32)
+    freq = jnp.asarray(np.tile(freq, 128 // freq.size).reshape(1, 128))
+    cfg = dict(n_kt=4, lat_dim=lat_dim, group=16, pitch=n_seqs + 8, in_flight=4, behind=2)
     n_k, n_blk = 8, 8
     dq_cols, dkv_cols = q_rank // 2, lat_dim // 2 + rope_dim
     blk = w_uq.shape[1] // 2 // n_blk
@@ -173,10 +193,9 @@
         out_shape=(
             jax.ShapeDtypeStruct((n_seqs, heads, lat_dim + 128), bf16),
             jax.ShapeDtypeStruct((n_seqs, lat_dim + 128), f32),
-            jax.ShapeDtypeStruct((n_seqs, lat_dim + rope_dim), bf16),
         ),
-        in_specs=[VMEM, ANY, ANY, ANY, ANY, VMEM, VMEM, VMEM, VMEM],
-        out_specs=(VMEM, VMEM, VMEM),
+        in_specs=[SMEM, VMEM, ANY, ANY, ANY, ANY, VMEM, VMEM, VMEM],
+        out_specs=(VMEM, VMEM),
         scratch_shapes=[
             pltpu.VMEM((n_k, d_model // n_k, dq_cols), bf16),
             pltpu.VMEM((dkv_cols, d_model), bf16),
@@ -185,16 +204,16 @@
             pltpu.VMEM((2, n_seqs, dq_cols + lat_dim // 2 + 128), f32),
             pltpu.VMEM((n_blk, n_seqs, blk), f32),
             pltpu.VMEM((n_blk, n_seqs, blk), f32),
-            pltpu.VMEM((lat_dim // 128 + 1, cfg["group"] * n_seqs, 128), f32),
+            pltpu.VMEM((2, lat_dim // 128 + 1, cfg["group"] * cfg["pitch"], 128), f32),
             dma((n_k,)), dma((cfg["n_kt"],)), dma((n_blk,)), dma((heads // cfg["group"],)),
             dma, dma, dma((n_blk,)), dma((n_blk,)),
         ],
         compiler_params=pltpu.CompilerParams(collective_id=1, has_side_effects=True, vmem_limit_bytes=56 * 1024 * 1024),
         name="project",
-    )(hidden, w_dq, w_dkv.T, w_uq, w_uk, q_gain.reshape(1, -1), kv_gain.reshape(1, -1), cos_t, sin_t)
-
-
-def attend_kernel(cfg, len_ref, q_ref, kvn_ref, ckv_hbm, kpe_hbm, cout_hbm, kout_hbm, o_hbm,
+    )(cache_len, hidden, w_dq, w_dkv.T, w_uq, w_uk, q_gain, kv_gain, freq)
+
+
+def attend_kernel(cfg, len_ref, q_ref, kvn_ref, ckv_hbm, kpe_hbm, cout_hbm, kout_hbm, o_hbm, kv_new,
                   cbuf, kbuf, obuf, peaks, denoms, isem, osem, psem):
     n_seqs, shard_len = ckv_hbm.shape[0], ckv_hbm.shape[1]
     lat_dim = ckv_hbm.shape[2]
@@ -220,6 +239,7 @@
     for i in range(n_buf - lag):
         for c in copies_in(i, i):
             c.start()
+    kv_new[...] = kvn_ref[:, :lat_dim + rope_dim].astype(kv_new.dtype)
     peaks[...] = jnp.zeros_like(peaks)
     denoms[...] = jnp.zeros_like(denoms)
 
@@ -313,9 +333,10 @@
             jax.ShapeDtypeStruct(ckv_blk.shape, ckv_blk.dtype),
             jax.ShapeDtypeStruct(kpe_blk_t.shape, kpe_blk_t.dtype),
             jax.ShapeDtypeStruct(terms_shape, jnp.float32),
+            jax.ShapeDtypeStruct((n_seqs, lat_dim + rope_dim), ckv_blk.dtype),
         ),
         in_specs=[SMEM, VMEM, VMEM, ANY, ANY],
-        out_specs=(ANY, ANY, ANY),
+        out_specs=(ANY, ANY, ANY, VMEM),
         scratch_shapes=[
             pltpu.VMEM((cfg["n_buf"], shard_len, lat_dim), ckv_blk.dtype),
             pltpu.VMEM((cfg["n_buf"], rope_dim, shard_len), kpe_blk_t.dtype),
@@ -353,7 +374,6 @@
     for k in order:
         loads[k].start()
     load_uv.start()
-    load_wo.start()
 
     others = ((0, 1), (1, 0), (2, 0), (3, 0))
     barrier = pltpu.get_barrier_semaphore()
@@ -395,6 +415,7 @@
     merge_pair(1, 1)
     merge_pair(0, 0)
     merge_pair(0, 1)
+    load_wo.start()
     x_sends[0].wait_recv()
     merge(own.at[2, 0], from_x.at[0], 0)
     y_sends[0].wait_recv()
@@ -423,51 +444,72 @@
         oheads[:, h * o_h.shape[1]:(h + 1) * o_h.shape[1]] = o_h.astype(jnp.bfloat16)
     load_wo.wait()
 
-    def partial_out(dev):
-        cols = pl.ds(pl.multiple_of(dev * width, 128), width)
-        return jnp.dot(oheads[...], wo[:, cols], preferred_element_type=jnp.float32)
-
+    def columns(dev, part):
+        at, size = parts[part]
+        return pl.ds(pl.multiple_of(dev * width + at, 128), size)
+
+    def partial_out(dev, part):
+        return jnp.dot(oheads[...], wo[:, columns(dev, part)], preferred_element_type=jnp.float32)
+
+    parts = ((0, width // 256 * 128), (width // 256 * 128, width - width // 256 * 128))
+    far = (3, 1, 2)
+    p_sends, i_sends, a_sends, f_sends = {}, {}, {}, {}
+
+    def start(waiting):
+        while waiting:
+            waiting.pop().start()
+
+    def put(ref, part, value):
+        ref[:, parts[part][0]:sum(parts[part])] = value
+
+    def get(ref, part):
+        return ref[:, parts[part][0]:sum(parts[part])]
+
+    def cut(ref, part):
+        return ref.at[:, pl.ds(*parts[part])]
+
+    mine = []
     waiting = []
-    p_sends, i_sends = {}, []
-    for q in (3, 1, 2, 0):
-        psend[q] = partial_out(device(q, 1))
-        p_sends[q] = send(psend.at[q], precv.at[q], p_ss.at[q], p_rs.at[q], device(0, 1))
-        for w in waiting:
-            w.start()
-        waiting = [p_sends[q]]
-    mine = None
-    for q in (3, 1, 2, 0):
-        part = partial_out(device(q, 0))
-        for w in waiting:
-            w.start()
-        waiting = []
-        p_sends[q].wait_recv()
-        if q:
-            isend[q - 1] = part + precv[q]
-            i_sends.append(send(isend.at[q - 1], irecv.at[q - 1], i_ss.at[q - 1], i_rs.at[q - 1], device(q, 0)))
-            waiting = [i_sends[-1]]
-        else:
-            mine = part + precv[0]
-    for s in i_sends:
-        s.wait_recv()
-    result = mine + irecv[0] + irecv[1] + irecv[2]
-    fin[...] = result
-    out_ref[:, pl.ds(pl.multiple_of(me * width, 128), width)] = result.astype(out_ref.dtype)
-
-    a_sends = {q: send(fin, agr.at[q - 1], a_ss.at[q - 1], a_rs.at[q - 1], device(q, 0)) for q in (3, 1, 2)}
-    f_sends = {0: send(fin, agp.at[0], f_ss.at[0], f_rs.at[0], device(0, 1))}
-    for q in (3, 1, 2):
-        a_sends[q].start()
-    f_sends[0].start()
-    for q in (1, 2, 3):
-        f_sends[q] = send(agr.at[q - 1], agp.at[q], f_ss.at[q], f_rs.at[q], device(0, 1))
-        a_sends[q].wait_recv()
-        f_sends[q].start()
-        out_ref[:, pl.ds(pl.multiple_of(device(q, 0) * width, 128), width)] = agr[q - 1].astype(out_ref.dtype)
-    for q in range(4):
-        f_sends[q].wait_recv()
-        out_ref[:, pl.ds(pl.multiple_of(device(q, 1) * width, 128), width)] = agp[q].astype(out_ref.dtype)
-    for s in list(d_sends.values()) + x_sends + y_sends + list(p_sends.values()) + i_sends + list(a_sends.values()) + list(f_sends.values()):
+    for part in range(2):
+        for q in far + (0,):
+            put(psend.at[q], part, partial_out(device(q, 1), part))
+            start(waiting)
+            p_sends[q, part] = send(cut(psend.at[q], part), cut(precv.at[q], part), p_ss.at[q, part], p_rs.at[q, part], device(0, 1))
+            waiting.append(p_sends[q, part])
+        for q in far + (0,):
+            value = partial_out(device(q, 0), part)
+            start(waiting)
+            p_sends[q, part].wait_recv()
+            value = value + get(precv.at[q], part)
+            if q:
+                put(isend.at[q - 1], part, value)
+                i_sends[q, part] = send(cut(isend.at[q - 1], part), cut(irecv.at[q - 1], part), i_ss.at[q - 1, part], i_rs.at[q - 1, part], device(q, 0))
+                waiting.append(i_sends[q, part])
+            else:
+                mine.append(value)
+        start(waiting)
+    for part in range(2):
+        for q in far:
+            i_sends[q, part].wait_recv()
+        result = mine[part] + get(irecv.at[0], part) + get(irecv.at[1], part) + get(irecv.at[2], part)
+        put(fin, part, result)
+        out_ref[:, columns(me, part)] = result
+        for q in far:
+            a_sends[q, part] = send(cut(fin, part), cut(agr.at[q - 1], part), a_ss.at[q - 1, part], a_rs.at[q - 1, part], device(q, 0))
+            a_sends[q, part].start()
+        f_sends[0, part] = send(cut(fin, part), cut(agp.at[0], part), f_ss.at[0, part], f_rs.at[0, part], device(0, 1))
+        f_sends[0, part].start()
+    for part in range(2):
+        for q in (1, 2, 3):
+            a_sends[q, part].wait_recv()
+            f_sends[q, part] = send(cut(agr.at[q - 1], part), cut(agp.at[q], part), f_ss.at[q, part], f_rs.at[q, part], device(0, 1))
+            f_sends[q, part].start()
+            out_ref[:, columns(device(q, 0), part)] = get(agr.at[q - 1], part)
+    for part in range(2):
+        for q in range(4):
+            f_sends[q, part].wait_recv()
+            out_ref[:, columns(device(q, 1), part)] = get(agp.at[q], part)
+    for s in list(d_sends.values()) + x_sends + y_sends + list(p_sends.values()) + list(i_sends.values()) + list(a_sends.values()) + list(f_sends.values()):
         s.wait_send()
 
 
@@ -480,7 +522,7 @@
     f32 = jnp.float32
     return pl.pallas_call(
         finish_kernel,
-        out_shape=jax.ShapeDtypeStruct((n_seqs, d_model), jnp.bfloat16),
+        out_shape=jax.ShapeDtypeStruct((n_seqs, d_model), f32),
         in_specs=[ANY, ANY, ANY],
         out_specs=VMEM,
         scratch_shapes=[
@@ -507,14 +549,14 @@
             pltpu.SemaphoreType.DMA((3,)),
             pltpu.SemaphoreType.DMA((3,)),
             pltpu.SemaphoreType.DMA((3,)),
-            pltpu.SemaphoreType.DMA((4,)),
-            pltpu.SemaphoreType.DMA((4,)),
-            pltpu.SemaphoreType.DMA((3,)),
-            pltpu.SemaphoreType.DMA((3,)),
-            pltpu.SemaphoreType.DMA((3,)),
-            pltpu.SemaphoreType.DMA((3,)),
-            pltpu.SemaphoreType.DMA((4,)),
-            pltpu.SemaphoreType.DMA((4,)),
+            pltpu.SemaphoreType.DMA((4, 2)),
+            pltpu.SemaphoreType.DMA((4, 2)),
+            pltpu.SemaphoreType.DMA((3, 2)),
+            pltpu.SemaphoreType.DMA((3, 2)),
+            pltpu.SemaphoreType.DMA((3, 2)),
+            pltpu.SemaphoreType.DMA((3, 2)),
+            pltpu.SemaphoreType.DMA((4, 2)),
+            pltpu.SemaphoreType.DMA((4, 2)),
         ],
         compiler_params=pltpu.CompilerParams(collective_id=0, has_side_effects=True, vmem_limit_bytes=56 * 1024 * 1024),
         name="finish",
@@ -525,10 +567,10 @@
     n_dev = mesh.shape['sp']
 
     def local_step(hidden, ckv_blk, kpe_blk, cache_len, w_dq, q_gain, w_uq, w_dkv, kv_gain, w_uk, w_uv, w_out):
-        q, kvn, kv_new = project(hidden, cache_len, w_dq, q_gain, w_uq, w_dkv, kv_gain, w_uk)
+        q, kvn = project(hidden, cache_len, w_dq, q_gain, w_uq, w_dkv, kv_gain, w_uk)
         qk_dim = w_uk.shape[1] + kpe_blk.shape[2]
-        ckv_out, kpe_out_t, terms = attend(q, kvn, cache_len, ckv_blk, jnp.swapaxes(kpe_blk, 1, 2), n_dev, qk_dim)
-        out = finish(terms, w_uv, w_out)
+        ckv_out, kpe_out_t, terms, kv_new = attend(q, kvn, cache_len, ckv_blk, jnp.swapaxes(kpe_blk, 1, 2), n_dev, qk_dim)
+        out = finish(terms, w_uv, w_out).astype(jnp.bfloat16)
         return out, ckv_out, jnp.swapaxes(kpe_out_t, 1, 2), kv_new
 
     cache_spec = P('dp', 'sp', None)

time: 137 us -> 123 us (0.90)
  Pallas kernels: 130 us -> 120 us
  local copies, waits for them, and re-layouts: 4.98 us -> 0 us
    pallas_call x1, Pallas kernels: 30.2 us -> 21.9 us  [project(): pl.pallas_call(functools.partial(project_kernel, cfg), out_shape=(jax.Sha...]
    reshape x2 -> x0, local copies, waits for them, and re-layouts: 2.55 us -> none  [the longest x1 1.28 us: project(): q_gain.reshape(1, -1)]
    unnamed x4 -> x0, local copies, waits for them, and re-layouts: 2.44 us -> none
    pallas_call x1, Pallas kernels: 45.5 us -> 43.5 us  [finish(): pl.pallas_call(finish_kernel, out_shape=jax.ShapeDtypeStruct((n_seqs, d_m...]
where the time goes in v3:
time: 123 us
  Pallas kernels  120 us (98%)
  other arithmetic  1.99 us (2%)
    pallas_call x1, Pallas kernels, attend(): pl.pallas_call(functools.partial(attend_kernel, cfg), out_shape=(jax.Shap...  54.6 us
    pallas_call x1, Pallas kernels, finish(): pl.pallas_call(finish_kernel, out_shape=jax.ShapeDtypeStruct((n_seqs, d_m...  43.5 us
    pallas_call x1, Pallas kernels, project(): pl.pallas_call(functools.partial(project_kernel, cfg), out_shape=(jax.Sha...  21.9 us

profile of v3, /device:TPU:0, one launch (start us, length us, event | category | flops | bytes accessed | tf_op | source)
XLA Modules:
  0.0 122.6 jit_solution(12924054494507030233)
XLA Ops:
  0.6 21.9 %project.1 = (bf16[32,64,640]{2,1,0:T(8,128)(2,1)}, f32[32,640]{1,0:T(8,128)}) custom-call(s32[32]{0:T(128)} %len_ref.3, bf16[32,7168]{1,0:T(8,128)(2,1)} %hidden.1, bf16[7168,1536]{1,0:T(8,128)(2,1)} %w_dq.1, bf16[576,7168]{1,0:T(8,128)(2,1)} %bitcast.4, bf16[1536,12288]{1,0:T(8,128)(2,1)} %w_uq.1, bf16[64,128,512]{2,1,0:T(8,128)(2,1)} %w_uk.1, ...), custom_call_target="tpu_custom_call" | custom-call | tf_op jit(solution)/shard_map/project/pallas_call | solution.py:191
  22.5 54.6 %attend.1 = (bf16[32,2048,512]{2,1,0:T(8,128)(2,1)}, bf16[32,64,2048]{2,1,0:T(8,128)(2,1)}, f32[8,2,17,8,512]{4,3,2,1,0:T(8,128)}, bf16[32,576]{1,0:T(8,128)(2,1)}) custom-call(s32[32]{0:T(128)} %len_ref.3, bf16[32,64,640]{2,1,0:T(8,128)(2,1)} %get-tuple-element.10.q_ref, f32[32,640]{1,0:T(8,128)} %get-tuple-element.11.kvn_ref, ...), custom_call_target="tpu_custom_call" | custom-call | tf_op jit(solution)/shard_map/attend/pallas_call | solution.py:330
  77.1 43.5 %finish.1 = f32[32,7168]{1,0:T(8,128)} custom-call(f32[8,2,17,8,512]{4,3,2,1,0:T(8,128)} %get-tuple-element.12.terms, bf16[64,128,512]{2,1,0:T(8,128)(2,1)} %w_uv.1, bf16[8192,7168]{1,0:T(8,128)(2,1)} %w_out.1), custom_call_target="tpu_custom_call" | custom-call | tf_op jit(solution)/shard_map/finish/pallas_call | solution.py:523
  120.6 2.0 %convert_element_type.3 = bf16[32,7168]{1,0:T(8,128)(2,1)} convert(f32[32,7168]{1,0:T(8,128)} %finish.1) | non-fusion elementwise | flops 229376 | bytes 1376256 | tf_op jit(solution)/shard_map/convert_element_type | solution.py:573

commit v4 on v3

--- a/solution.py
+++ b/solution.py
@@ -14,7 +14,7 @@
 MESH = pl.DeviceIdType.MESH
 VMEM = pl.BlockSpec(memory_space=pltpu.VMEM)
 SMEM = pl.BlockSpec(memory_space=pltpu.SMEM)
-ANY = pl.BlockSpec(memory_space=pl.ANY)
+HBM = pl.BlockSpec(memory_space=pltpu.HBM)
 
 
 def project_kernel(cfg, len_ref, hidden, w_dq, w_dkv_t, w_uq, w_uk, q_gain_ref, kv_gain_ref, freq, q_out, kvn_out,
@@ -194,7 +194,7 @@
             jax.ShapeDtypeStruct((n_seqs, heads, lat_dim + 128), bf16),
             jax.ShapeDtypeStruct((n_seqs, lat_dim + 128), f32),
         ),
-        in_specs=[SMEM, VMEM, ANY, ANY, ANY, ANY, VMEM, VMEM, VMEM],
+        in_specs=[SMEM, VMEM, HBM, HBM, HBM, HBM, VMEM, VMEM, VMEM],
         out_specs=(VMEM, VMEM),
         scratch_shapes=[
             pltpu.VMEM((n_k, d_model // n_k, dq_cols), bf16),
@@ -208,17 +208,17 @@
             dma((n_k,)), dma((cfg["n_kt"],)), dma((n_blk,)), dma((heads // cfg["group"],)),
             dma, dma, dma((n_blk,)), dma((n_blk,)),
         ],
-        compiler_params=pltpu.CompilerParams(collective_id=1, has_side_effects=True, vmem_limit_bytes=56 * 1024 * 1024),
+        compiler_params=pltpu.CompilerParams(collective_id=1, has_side_effects=True, vmem_limit_bytes=48 * 1024 * 1024),
         name="project",
     )(cache_len, hidden, w_dq, w_dkv.T, w_uq, w_uk, q_gain, kv_gain, freq)
 
 
-def attend_kernel(cfg, len_ref, q_ref, kvn_ref, ckv_hbm, kpe_hbm, cout_hbm, kout_hbm, o_hbm, kv_new,
-                  cbuf, kbuf, obuf, peaks, denoms, isem, osem, psem):
+def attend_kernel(cfg, len_ref, q_ref, kvn_ref, ckv_hbm, kpe_hbm, cout_hbm, kout_hbm, terms, kv_new,
+                  cbuf, kbuf, peaks, denoms, isem, osem):
     n_seqs, shard_len = ckv_hbm.shape[0], ckv_hbm.shape[1]
     lat_dim = ckv_hbm.shape[2]
     rope_dim = kpe_hbm.shape[1]
-    per = o_hbm.shape[2] - 1
+    per = terms.shape[2] - 1
     n_buf, lag, chunk = cfg["n_buf"], cfg["lag"], cfg["chunk"]
     base = lax.axis_index('sp') * shard_len
 
@@ -229,12 +229,6 @@
     def copies_out(b, slot):
         return (pltpu.make_async_copy(cbuf.at[slot], cout_hbm.at[b], osem.at[slot, 0]),
                 pltpu.make_async_copy(kbuf.at[slot], kout_hbm.at[b], osem.at[slot, 1]))
-
-    def copy_terms(b, side):
-        return pltpu.make_async_copy(obuf.at[side], o_hbm.at[:, b // per, b % per], psem.at[side])
-
-    def copy_stats(part):
-        return pltpu.make_async_copy(obuf.at[0], o_hbm.at[:, part, per], psem.at[part])
 
     for i in range(n_buf - lag):
         for c in copies_in(i, i):
@@ -294,31 +288,19 @@
             lat_sum = term if lat_sum is None else lat_sum + term
         for c in copies_out(b, slot):
             c.start()
-        side = lax.rem(b, 2)
-
-        @pl.when(b >= 2)
-        def _():
-            copy_terms(b - 2, side).wait()
-
-        obuf[side] = lat_sum.reshape(obuf.shape[1:])
+        terms[:, b // per, b % per] = lat_sum.reshape(terms.shape[0], *terms.shape[3:])
         lane = lax.broadcasted_iota(jnp.int32, peaks.shape, 1)
         peaks[...] = jnp.where(lane == b, peak, peaks[...])
         denoms[...] = jnp.where(lane == b, denom, denoms[...])
-        copy_terms(b, side).start()
         return carry
 
     lax.fori_loop(0, n_seqs, step, 0)
-    for i in range(n_seqs - 2, n_seqs):
-        copy_terms(i, i % 2).wait()
-    obuf[0, :, :, 0:128] = peaks[...].reshape(obuf.shape[1], obuf.shape[2], 128)
-    obuf[0, :, :, 128:256] = denoms[...].reshape(obuf.shape[1], obuf.shape[2], 128)
+    for part in range(2):
+        terms[:, part, per, :, :128] = peaks[...].reshape(terms.shape[0], terms.shape[3], 128)
+        terms[:, part, per, :, 128:256] = denoms[...].reshape(terms.shape[0], terms.shape[3], 128)
     for i in range(n_seqs - lag, n_seqs):
         for c in copies_out(i, i % n_buf):
             c.wait()
-    for part in range(2):
-        copy_stats(part).start()
-    for part in range(2):
-        copy_stats(part).wait()
 
 
 def attend(q, kvn, cache_len, ckv_blk, kpe_blk_t, n_dev, qk_dim):
@@ -335,19 +317,17 @@
             jax.ShapeDtypeStruct(terms_shape, jnp.float32),
             jax.ShapeDtypeStruct((n_seqs, lat_dim + rope_dim), ckv_blk.dtype),
         ),
-        in_specs=[SMEM, VMEM, VMEM, ANY, ANY],
-        out_specs=(ANY, ANY, ANY, VMEM),
+        in_specs=[SMEM, VMEM, VMEM, HBM, HBM],
+        out_specs=(HBM, HBM, VMEM, VMEM),
         scratch_shapes=[
             pltpu.VMEM((cfg["n_buf"], shard_len, lat_dim), ckv_blk.dtype),
             pltpu.VMEM((cfg["n_buf"], rope_dim, shard_len), kpe_blk_t.dtype),
-            pltpu.VMEM((2, n_dev, n_heads // n_dev, lat_dim), jnp.float32),
             pltpu.VMEM((n_heads, 128), jnp.float32),
             pltpu.VMEM((n_heads, 128), jnp.float32),
             pltpu.SemaphoreType.DMA((cfg["n_buf"], 2)),
             pltpu.SemaphoreType.DMA((cfg["n_buf"], 2)),
-            pltpu.SemaphoreType.DMA((2,)),
         ],
-        compiler_params=pltpu.CompilerParams(vmem_limit_bytes=56 * 1024 * 1024),
+        compiler_params=pltpu.CompilerParams(vmem_limit_bytes=44 * 1024 * 1024),
         name="attend",
     )(cache_len, q, kvn, ckv_blk, kpe_blk_t)
 
@@ -523,7 +503,7 @@
     return pl.pallas_call(
         finish_kernel,
         out_shape=jax.ShapeDtypeStruct((n_seqs, d_model), f32),
-        in_specs=[ANY, ANY, ANY],
+        in_specs=[VMEM, HBM, HBM],
         out_specs=VMEM,
         scratch_shapes=[
             pltpu.VMEM((4, 2, rows, heads, lat_dim), f32),
@@ -558,7 +538,7 @@
             pltpu.SemaphoreType.DMA((4, 2)),
             pltpu.SemaphoreType.DMA((4, 2)),
         ],
-        compiler_params=pltpu.CompilerParams(collective_id=0, has_side_effects=True, vmem_limit_bytes=56 * 1024 * 1024),
+        compiler_params=pltpu.CompilerParams(collective_id=0, has_side_effects=True, vmem_limit_bytes=48 * 1024 * 1024),
         name="finish",
     )(terms, w_uv, w_out)
 

time: 123 us -> 119 us (0.967)
  Pallas kernels: 120 us -> 114 us
  local copies, waits for them, and re-layouts: 0 us -> 3.69 us
    unnamed x0 -> x12, local copies, waits for them, and re-layouts: none -> 3.69 us
    pallas_call x1, Pallas kernels: 54.6 us -> 51.1 us  [attend(): pl.pallas_call(functools.partial(attend_kernel, cfg), out_shape=(jax.Shap...]
    pallas_call x1, Pallas kernels: 21.9 us -> 19.8 us  [project(): pl.pallas_call(functools.partial(project_kernel, cfg), out_shape=(jax.Sha...]
where the time goes in v4:
time: 119 us
  Pallas kernels  114 us (96%)
  local copies, waits for them, and re-layouts  3.69 us (3%)
    pallas_call x1, Pallas kernels, attend(): pl.pallas_call(functools.partial(attend_kernel, cfg), out_shape=(jax.Shap...  51.1 us
    pallas_call x1, Pallas kernels, finish(): pl.pallas_call(finish_kernel, out_shape=jax.ShapeDtypeStruct((n_seqs, d_m...  42.9 us
    pallas_call x1, Pallas kernels, project(): pl.pallas_call(functools.partial(project_kernel, cfg), out_shape=(jax.Sha...  19.8 us
    unnamed x12, local copies, waits for them, and re-layouts  3.69 us

profile of v4, /device:TPU:0, one launch (start us, length us, event | category | flops | bytes accessed | tf_op | source)
XLA Modules:
  0.0 119.0 jit_solution(13072806456003051609)
XLA Ops:
  0.6 0.0 copy-start
  0.6 1.0 copy-done
  1.7 0.0 copy-start.1
  1.7 0.7 copy-done.1
  2.3 0.0 copy-start.2
  2.3 0.7 copy-done.2
  3.0 0.0 copy-start.4
  3.0 0.7 copy-done.4
  3.7 0.0 copy-start.5
  3.7 0.7 copy-done.5
  4.3 0.0 copy-start.3
  4.3 19.8 %project.1 = (bf16[32,64,640]{2,1,0:T(8,128)(2,1)S(1)}, f32[32,640]{1,0:T(8,128)S(1)}) custom-call(s32[32]{0:T(128)S(1)} %copy-done.2, bf16[32,7168]{1,0:T(8,128)(2,1)S(1)} %copy-done, bf16[7168,1536]{1,0:T(8,128)(2,1)} %w_dq.1, bf16[576,7168]{1,0:T(8,128)(2,1)} %bitcast.4, bf16[1536,12288]{1,0:T(8,128)(2,1)} %w_uq.1, bf16[64,128,512]{2,1,0:T(8,128)(2,1)} %w_uk.1, ...), custom_call_target="tpu_custom_call" | custom-call | tf_op jit(solution)/shard_map/project/pallas_call | solution.py:191
  24.2 0.0 copy-done.3
  24.2 51.1 %attend.1 = (bf16[32,2048,512]{2,1,0:T(8,128)(2,1)}, bf16[32,64,2048]{2,1,0:T(8,128)(2,1)}, f32[8,2,17,8,512]{4,3,2,1,0:T(8,128)S(1)}, bf16[32,576]{1,0:T(8,128)(2,1)}) custom-call(s32[32]{0:T(128)S(1)} %copy-done.3, bf16[32,64,640]{2,1,0:T(8,128)(2,1)S(1)} %get-tuple-element.10.q_ref, f32[32,640]{1,0:T(8,128)S(1)} %get-tuple-element.11.kvn_ref, ...), custom_call_target="tpu_custom_call" | custom-call | tf_op jit(solution)/shard_map/attend/pallas_call | solution.py:312
  75.3 42.9 %finish.1 = f32[32,7168]{1,0:T(8,128)S(1)} custom-call(f32[8,2,17,8,512]{4,3,2,1,0:T(8,128)S(1)} %get-tuple-element.12.terms, bf16[64,128,512]{2,1,0:T(8,128)(2,1)} %w_uv.1, bf16[8192,7168]{1,0:T(8,128)(2,1)} %w_out.1), custom_call_target="tpu_custom_call" | custom-call | tf_op jit(solution)/shard_map/finish/pallas_call | solution.py:503
  118.2 0.8 convert_element_type.3
Async XLA Ops:
  0.6 1.0 copy-start
  1.7 0.7 copy-start.1
  2.3 0.7 copy-start.2
  3.0 0.7 copy-start.4
  3.7 0.7 copy-start.5
  4.3 19.8 %copy-start.3 = (s32[32]{0:T(128)S(1)}, s32[32]{0:T(128)}, u32[]{:S(2)}) copy-start(s32[32]{0:T(128)} %len_ref.3) | copy-start | bytes 388

commit v5 on v4

--- a/solution.py
+++ b/solution.py
@@ -17,7 +17,7 @@
 HBM = pl.BlockSpec(memory_space=pltpu.HBM)
 
 
-def project_kernel(cfg, len_ref, hidden, w_dq, w_dkv_t, w_uq, w_uk, q_gain_ref, kv_gain_ref, freq, q_out, kvn_out,
+def project_kernel(cfg, small_ref, hidden, w_dq, w_dkv_t, w_uq, w_uk, q_out, kvn_out,
                    dq, dkv, uq, uk, halves, q_mine, q_theirs, turn, dq_sem, dkv_sem, uq_sem, uk_sem, h_ss, h_rs, q_ss, q_rs):
     n_seqs = hidden.shape[0]
     n_k, k_rows, dq_cols = dq.shape
@@ -78,14 +78,15 @@
 
     lane = lax.broadcasted_iota(jnp.int32, (n_seqs, 128), 1)
     row = lax.broadcasted_iota(jnp.int32, (n_seqs, 128), 0)
-    position = jnp.zeros((n_seqs, 128), f32)
-    for b in range(n_seqs):
-        position = jnp.where(row == b, len_ref[b].astype(f32), position)
-    angle = position * freq[...]
+    small = small_ref[...].reshape(1, -1)
+    q_gain, kv_gain, lengths = small[:, :2 * dq_cols], small[:, 2 * dq_cols:2 * dq_cols + lat_dim], small[:, 2 * dq_cols + lat_dim:]
+    position = jnp.sum(jnp.where(lane == row, lengths, 0.0), axis=1, keepdims=True)
+    freq = jnp.zeros((n_seqs, 128), f32)
+    for i, value in enumerate(cfg["freqs"]):
+        freq = jnp.where(lane % 32 == i, value, freq)
+    angle = position * freq
     cos_t = jnp.cos(angle)
     sin_t = jnp.where(lane % 64 < 32, -jnp.sin(angle), jnp.sin(angle))
-    q_gain = q_gain_ref[...].astype(f32).reshape(1, -1)
-    kv_gain = kv_gain_ref[...].astype(f32).reshape(1, -1)
 
     acc_q = jnp.zeros((n_seqs, dq_cols), f32)
     acc_kv = jnp.zeros((n_seqs, dkv_cols), f32)
@@ -180,13 +181,13 @@
     heads, nope_dim, lat_dim = w_uk.shape
     q_rank = w_dq.shape[1]
     rope_dim = w_dkv.shape[1] - lat_dim
-    freq = np.power(ROPE_THETA, -2.0 * np.arange(rope_dim // 2) / rope_dim).astype(np.float32)
-    freq = jnp.asarray(np.tile(freq, 128 // freq.size).reshape(1, 128))
-    cfg = dict(n_kt=4, lat_dim=lat_dim, group=16, pitch=n_seqs + 8, in_flight=4, behind=2)
+    freqs = [float(f) for f in np.power(ROPE_THETA, -2.0 * np.arange(rope_dim // 2) / rope_dim).astype(np.float32)]
+    cfg = dict(n_kt=4, lat_dim=lat_dim, group=16, pitch=n_seqs + 8, in_flight=4, behind=2, freqs=freqs)
     n_k, n_blk = 8, 8
     dq_cols, dkv_cols = q_rank // 2, lat_dim // 2 + rope_dim
     blk = w_uq.shape[1] // 2 // n_blk
     f32, bf16 = jnp.float32, jnp.bfloat16
+    small = jnp.concatenate([q_gain.astype(f32), kv_gain.astype(f32), cache_len.astype(f32), jnp.zeros((128 - n_seqs,), f32)])
     dma = pltpu.SemaphoreType.DMA
     return pl.pallas_call(
         functools.partial(project_kernel, cfg),
@@ -194,7 +195,7 @@
             jax.ShapeDtypeStruct((n_seqs, heads, lat_dim + 128), bf16),
             jax.ShapeDtypeStruct((n_seqs, lat_dim + 128), f32),
         ),
-        in_specs=[SMEM, VMEM, HBM, HBM, HBM, HBM, VMEM, VMEM, VMEM],
+        in_specs=[VMEM, VMEM, HBM, HBM, HBM, HBM],
         out_specs=(VMEM, VMEM),
         scratch_shapes=[
             pltpu.VMEM((n_k, d_model // n_k, dq_cols), bf16),
@@ -210,7 +211,7 @@
         ],
         compiler_params=pltpu.CompilerParams(collective_id=1, has_side_effects=True, vmem_limit_bytes=48 * 1024 * 1024),
         name="project",
-    )(cache_len, hidden, w_dq, w_dkv.T, w_uq, w_uk, q_gain, kv_gain, freq)
+    )(small, hidden, w_dq, w_dkv.T, w_uq, w_uk)
 
 
 def attend_kernel(cfg, len_ref, q_ref, kvn_ref, ckv_hbm, kpe_hbm, cout_hbm, kout_hbm, terms, kv_new,
@@ -327,7 +328,7 @@
             pltpu.SemaphoreType.DMA((cfg["n_buf"], 2)),
             pltpu.SemaphoreType.DMA((cfg["n_buf"], 2)),
         ],
-        compiler_params=pltpu.CompilerParams(vmem_limit_bytes=44 * 1024 * 1024),
+        compiler_params=pltpu.CompilerParams(vmem_limit_bytes=36 * 1024 * 1024),
         name="attend",
     )(cache_len, q, kvn, ckv_blk, kpe_blk_t)
 

time: 119 us -> 118 us (level)
  local copies, waits for them, and re-layouts: 3.69 us -> 2.47 us
    unnamed x12 -> x6, local copies, waits for them, and re-layouts: 3.69 us -> 1.03 us
    pallas_call x1, Pallas kernels: 51.1 us -> 48.9 us  [attend(): pl.pallas_call(functools.partial(attend_kernel, cfg), out_shape=(jax.Shap...]
    concatenate x0 -> x1, local copies, waits for them, and re-layouts: none -> 1.45 us  [project(): jnp.concatenate([q_gain.astype(f32), kv_gain.astype(f32), cache_len.astyp...]
where the time goes in v5:
time: 118 us; the launch traced here: 117 us
  Pallas kernels  113 us (96%)
  local copies, waits for them, and re-layouts  2.47 us (2%)
  other arithmetic  1.47 us (1%)
    pallas_call x1, Pallas kernels, attend(): pl.pallas_call(functools.partial(attend_kernel, cfg), out_shape=(jax.Shap...  48.9 us
    pallas_call x1, Pallas kernels, finish(): pl.pallas_call(finish_kernel, out_shape=jax.ShapeDtypeStruct((n_seqs, d_m...  43 us
    pallas_call x1, Pallas kernels, project(): pl.pallas_call(functools.partial(project_kernel, cfg), out_shape=(jax.Sha...  20.9 us

profile of v5, /device:TPU:0, one launch (start us, length us, event | category | flops | bytes accessed | tf_op | source)
XLA Modules:
  0.0 117.5 jit_solution(3835648095143834228)
XLA Ops:
  0.6 0.7 convert_element_type.14
  1.3 1.4 %concatenate.3.small_ref = f32[2176]{0:T(1024)S(1)} concatenate(bf16[1536]{0:T(1024)(128)(2,1)} %param.17, bf16[512]{0:T(512)(128)(2,1)} %param.20, f32[32]{0:T(128)S(1)} %convert_element_type.14, f32[96]{0:T(128)S(1)} %broadcast_in_dim.3), dimensions={0} | concatenate | bytes 13312 | tf_op jit(solution)/shard_map/concatenate | solution.py:190
  2.7 0.0 copy-start.1
  2.7 1.0 copy-done.1
  3.8 0.0 copy-start
  3.8 0.0 copy-start.2
  3.8 20.9 %project.1 = (bf16[32,64,640]{2,1,0:T(8,128)(2,1)S(1)}, f32[32,640]{1,0:T(8,128)S(1)}) custom-call(f32[2176]{0:T(1024)S(1)} %concatenate.3.small_ref, bf16[32,7168]{1,0:T(8,128)(2,1)S(1)} %copy-done.1, bf16[7168,1536]{1,0:T(8,128)(2,1)} %w_dq.1, bf16[576,7168]{1,0:T(8,128)(2,1)} %bitcast.4, bf16[1536,12288]{1,0:T(8,128)(2,1)} %w_uq.1, bf16[64,128,512]{2,1,0:T(8,128)(2,1)} %w_uk.1), custom_call_target="tpu_custom_call" | custom-call | tf_op jit(solution)/shard_map/project/pallas_call | solution.py:192
  24.7 0.0 copy-done
  24.7 0.0 copy-done.2
  24.7 48.9 %attend.1 = (bf16[32,2048,512]{2,1,0:T(8,128)(2,1)}, bf16[32,64,2048]{2,1,0:T(8,128)(2,1)}, f32[8,2,17,8,512]{4,3,2,1,0:T(8,128)S(1)}, bf16[32,576]{1,0:T(8,128)(2,1)}) custom-call(s32[32]{0:T(128)S(1)} %copy-done.2, bf16[32,64,640]{2,1,0:T(8,128)(2,1)S(1)} %get-tuple-element.10.q_ref, f32[32,640]{1,0:T(8,128)S(1)} %get-tuple-element.11.kvn_ref, ...), custom_call_target="tpu_custom_call" | custom-call | tf_op jit(solution)/shard_map/attend/pallas_call | solution.py:313
  73.6 43.0 %finish.1 = f32[32,7168]{1,0:T(8,128)S(1)} custom-call(f32[8,2,17,8,512]{4,3,2,1,0:T(8,128)S(1)} %get-tuple-element.12.terms, bf16[64,128,512]{2,1,0:T(8,128)(2,1)} %w_uv.1, bf16[8192,7168]{1,0:T(8,128)(2,1)} %w_out.1), custom_call_target="tpu_custom_call" | custom-call | tf_op jit(solution)/shard_map/finish/pallas_call | solution.py:504
  116.6 0.8 convert_element_type.15
  (1 shorter events, 0.0 us)
Async XLA Ops:
  2.7 1.0 copy-start.1
  3.8 20.9 %copy-start = (bf16[32,2048,64]{1,2,0:T(8,128)(2,1)S(1)}, bf16[32,2048,64]{1,2,0:T(8,128)(2,1)}, u32[]{:S(2)}) copy-start(bf16[32,2048,64]{1,2,0:T(8,128)(2,1)} %param.14) | copy-start | bytes 25165828
  3.8 20.9 %copy-start.2 = (s32[32]{0:T(128)S(1)}, s32[32]{0:T(128)}, u32[]{:S(2)}) copy-start(s32[32]{0:T(128)} %len_ref.1) | copy-start | bytes 388

commit v6 on v5

--- a/solution.py
+++ b/solution.py
@@ -187,7 +187,11 @@
     dq_cols, dkv_cols = q_rank // 2, lat_dim // 2 + rope_dim
     blk = w_uq.shape[1] // 2 // n_blk
     f32, bf16 = jnp.float32, jnp.bfloat16
-    small = jnp.concatenate([q_gain.astype(f32), kv_gain.astype(f32), cache_len.astype(f32), jnp.zeros((128 - n_seqs,), f32)])
+    at, small = 0, 0.0
+    n_small = q_rank + lat_dim + 128
+    for piece in (q_gain, kv_gain, cache_len):
+        small = small + jnp.pad(piece, (at, n_small - at - piece.size)).astype(f32)
+        at += piece.size
     dma = pltpu.SemaphoreType.DMA
     return pl.pallas_call(
         functools.partial(project_kernel, cfg),
@@ -334,7 +338,7 @@
 
 
 def finish_kernel(terms, w_uv, w_out, out_ref, own, pair, from_x, from_y, uv, wo, merged, oheads, psend, precv, isend, irecv, fin, agr, agp,
-                  lsem, own_sem, d_ss, d_rs, x_ss, x_rs, y_ss, y_rs, p_ss, p_rs, i_ss, i_rs, a_ss, a_rs, f_ss, f_rs):
+                  lsem, d_ss, d_rs, x_ss, x_rs, y_ss, y_rs, p_ss, p_rs, i_ss, i_rs, a_ss, a_rs, f_ss, f_rs):
     n_seqs, width = fin.shape
     heads = uv.shape[0]
     depth = wo.shape[0]
@@ -351,9 +355,6 @@
     load_wo = pltpu.make_async_copy(w_out.at[pl.ds(me * depth, depth)], wo, lsem.at[1])
     order = ((3, 0), (3, 1), (1, 0), (2, 1), (2, 0), (1, 1), (0, 0), (0, 1))
     per = n_seqs // 2
-    loads = {(q, h): pltpu.make_async_copy(terms.at[device(q, 0), h], own.at[q, h], own_sem.at[q, h]) for q, h in order}
-    for k in order:
-        loads[k].start()
     load_uv.start()
 
     others = ((0, 1), (1, 0), (2, 0), (3, 0))
@@ -366,20 +367,20 @@
     for k in order:
         d_sends[k].start()
 
-    def merge(dst, src, h):
-        old, new = dst[per, :, :128], src[per, :, :128]
+    def merge(dst, src, h, first=None):
+        base = dst if first is None else first
+        old, new = base[per, :, :128], src[per, :, :128]
         peak = jnp.maximum(old, new)
         f_old, f_new = jnp.exp(old - peak), jnp.exp(new - peak)
         dst[per, :, :128] = peak
-        dst[per, :, 128:256] = f_old * dst[per, :, 128:256] + f_new * src[per, :, 128:256]
+        dst[per, :, 128:256] = f_old * base[per, :, 128:256] + f_new * src[per, :, 128:256]
         for i in range(per):
             b = h * per + i
-            dst[i] = f_old[:, b:b + 1] * dst[i] + f_new[:, b:b + 1] * src[i]
+            dst[i] = f_old[:, b:b + 1] * base[i] + f_new[:, b:b + 1] * src[i]
 
     def merge_pair(q, h):
-        loads[q, h].wait()
         d_sends[q, h].wait_recv()
-        merge(own.at[q, h], pair.at[q, h], h)
+        merge(own.at[q, h], pair.at[q, h], h, terms.at[device(q, 0), h])
 
     x_dev, y_dev = device(1, 0), device(2, 0)
     x_sends = [send(own.at[k], from_x.at[i], x_ss.at[i], x_rs.at[i], x_dev) for i, k in enumerate(((3, 0), (1, 0), (1, 1)))]
@@ -525,7 +526,6 @@
             pltpu.SemaphoreType.DMA((2,)),
             pltpu.SemaphoreType.DMA((4, 2)),
             pltpu.SemaphoreType.DMA((4, 2)),
-            pltpu.SemaphoreType.DMA((4, 2)),
             pltpu.SemaphoreType.DMA((3,)),
             pltpu.SemaphoreType.DMA((3,)),
             pltpu.SemaphoreType.DMA((3,)),

time: 118 us -> 116 us (0.983)
  local copies, waits for them, and re-layouts: 2.47 us -> 1.03 us
    concatenate x1 -> x0, local copies, waits for them, and re-layouts: 1.45 us -> none  [project(): jnp.concatenate([q_gain.astype(f32), kv_gain.astype(f32), cache_len.astyp...]
where the time goes in v6:
time: 116 us
  Pallas kernels  112 us (97%)
  other arithmetic  1.54 us (1%)
    pallas_call x1, Pallas kernels, attend(): pl.pallas_call(functools.partial(attend_kernel, cfg), out_shape=(jax.Shap...  48.9 us
    pallas_call x1, Pallas kernels, finish(): pl.pallas_call(finish_kernel, out_shape=jax.ShapeDtypeStruct((n_seqs, d_m...  42.6 us
    pallas_call x1, Pallas kernels, project(): pl.pallas_call(functools.partial(project_kernel, cfg), out_shape=(jax.Sha...  20.9 us

profile of v6, /device:TPU:0, one launch (start us, length us, event | category | flops | bytes accessed | tf_op | source)
XLA Modules:
  0.0 115.7 jit_solution(6640076173495664476)
XLA Ops:
  0.6 0.7 convert_add_fusion.small_ref
  1.4 0.0 copy-start.1
  1.4 1.0 copy-done.1
  2.4 0.0 copy-start
  2.4 0.0 copy-start.2
  2.4 20.9 %project.1 = (bf16[32,64,640]{2,1,0:T(8,128)(2,1)S(1)}, f32[32,640]{1,0:T(8,128)S(1)}) custom-call(f32[2176]{0:T(1024)S(1)} %convert_add_fusion.small_ref, bf16[32,7168]{1,0:T(8,128)(2,1)S(1)} %copy-done.1, bf16[7168,1536]{1,0:T(8,128)(2,1)} %w_dq.1, bf16[576,7168]{1,0:T(8,128)(2,1)} %bitcast.4, bf16[1536,12288]{1,0:T(8,128)(2,1)} %w_uq.1, ...), custom_call_target="tpu_custom_call" | custom-call | tf_op jit(solution)/shard_map/project/pallas_call | solution.py:196
  23.3 0.0 copy-done
  23.3 0.0 copy-done.2
  23.3 48.9 %attend.1 = (bf16[32,2048,512]{2,1,0:T(8,128)(2,1)}, bf16[32,64,2048]{2,1,0:T(8,128)(2,1)}, f32[8,2,17,8,512]{4,3,2,1,0:T(8,128)S(1)}, bf16[32,576]{1,0:T(8,128)(2,1)}) custom-call(s32[32]{0:T(128)S(1)} %copy-done.2, bf16[32,64,640]{2,1,0:T(8,128)(2,1)S(1)} %get-tuple-element.10.q_ref, f32[32,640]{1,0:T(8,128)S(1)} %get-tuple-element.11.kvn_ref, ...), custom_call_target="tpu_custom_call" | custom-call | tf_op jit(solution)/shard_map/attend/pallas_call | solution.py:317
  72.2 42.6 %finish.1 = f32[32,7168]{1,0:T(8,128)S(1)} custom-call(f32[8,2,17,8,512]{4,3,2,1,0:T(8,128)S(1)} %get-tuple-element.12.terms, bf16[64,128,512]{2,1,0:T(8,128)(2,1)} %w_uv.1, bf16[8192,7168]{1,0:T(8,128)(2,1)} %w_out.1), custom_call_target="tpu_custom_call" | custom-call | tf_op jit(solution)/shard_map/finish/pallas_call | solution.py:505
  114.9 0.8 convert_element_type.19
Async XLA Ops:
  1.4 1.0 copy-start.1
  2.4 20.9 %copy-start = (bf16[32,2048,64]{1,2,0:T(8,128)(2,1)S(1)}, bf16[32,2048,64]{1,2,0:T(8,128)(2,1)}, u32[]{:S(2)}) copy-start(bf16[32,2048,64]{1,2,0:T(8,128)(2,1)} %param.14) | copy-start | bytes 25165828
  2.4 20.9 %copy-start.2 = (s32[32]{0:T(128)S(1)}, s32[32]{0:T(128)}, u32[]{:S(2)}) copy-start(s32[32]{0:T(128)} %len_ref.1) | copy-start | bytes 388

commit v7 on v6

--- a/solution.py
+++ b/solution.py
@@ -182,7 +182,7 @@
     q_rank = w_dq.shape[1]
     rope_dim = w_dkv.shape[1] - lat_dim
     freqs = [float(f) for f in np.power(ROPE_THETA, -2.0 * np.arange(rope_dim // 2) / rope_dim).astype(np.float32)]
-    cfg = dict(n_kt=4, lat_dim=lat_dim, group=16, pitch=n_seqs + 8, in_flight=4, behind=2, freqs=freqs)
+    cfg = dict(n_kt=4, lat_dim=lat_dim, group=16, pitch=n_seqs + 8, in_flight=6, behind=2, freqs=freqs)
     n_k, n_blk = 8, 8
     dq_cols, dkv_cols = q_rank // 2, lat_dim // 2 + rope_dim
     blk = w_uq.shape[1] // 2 // n_blk
@@ -383,8 +383,26 @@
         merge(own.at[q, h], pair.at[q, h], h, terms.at[device(q, 0), h])
 
     x_dev, y_dev = device(1, 0), device(2, 0)
-    x_sends = [send(own.at[k], from_x.at[i], x_ss.at[i], x_rs.at[i], x_dev) for i, k in enumerate(((3, 0), (1, 0), (1, 1)))]
-    y_sends = [send(own.at[k], from_y.at[i], y_ss.at[i], y_rs.at[i], y_dev) for i, k in enumerate(((3, 1), (2, 1), (2, 0)))]
+
+    class Both:
+        def __init__(self, src, dst, ss, rs, dev):
+            body, tail = pl.ds(0, per), pl.ds(0, 256)
+            self.copies = (send(src.at[body], dst.at[body], ss.at[0], rs.at[0], dev), send(src.at[per, :, tail], dst.at[per, :, tail], ss.at[1], rs.at[1], dev))
+
+        def start(self):
+            for copy in self.copies:
+                copy.start()
+
+        def wait_recv(self):
+            for copy in self.copies:
+                copy.wait_recv()
+
+        def wait_send(self):
+            for copy in self.copies:
+                copy.wait_send()
+
+    x_sends = [Both(own.at[k], from_x.at[i], x_ss.at[i], x_rs.at[i], x_dev) for i, k in enumerate(((3, 0), (1, 0), (1, 1)))]
+    y_sends = [Both(own.at[k], from_y.at[i], y_ss.at[i], y_rs.at[i], y_dev) for i, k in enumerate(((3, 1), (2, 1), (2, 0)))]
     merge_pair(3, 0)
     merge_pair(3, 1)
     x_sends[0].start()
@@ -526,10 +544,10 @@
             pltpu.SemaphoreType.DMA((2,)),
             pltpu.SemaphoreType.DMA((4, 2)),
             pltpu.SemaphoreType.DMA((4, 2)),
-            pltpu.SemaphoreType.DMA((3,)),
-            pltpu.SemaphoreType.DMA((3,)),
-            pltpu.SemaphoreType.DMA((3,)),
-            pltpu.SemaphoreType.DMA((3,)),
+            pltpu.SemaphoreType.DMA((3, 2)),
+            pltpu.SemaphoreType.DMA((3, 2)),
+            pltpu.SemaphoreType.DMA((3, 2)),
+            pltpu.SemaphoreType.DMA((3, 2)),
             pltpu.SemaphoreType.DMA((4, 2)),
             pltpu.SemaphoreType.DMA((4, 2)),
             pltpu.SemaphoreType.DMA((3, 2)),

time: 116 us -> 113 us (0.974)
  Pallas kernels: 112 us -> 110 us
    pallas_call x1, Pallas kernels: 20.9 us -> 18.8 us  [project(): pl.pallas_call(functools.partial(project_kernel, cfg), out_shape=(jax.Sha...]
where the time goes in v7:
time: 113 us
  Pallas kernels  110 us (97%)
  other arithmetic  1.54 us (1%)
    pallas_call x1, Pallas kernels, attend(): pl.pallas_call(functools.partial(attend_kernel, cfg), out_shape=(jax.Shap...  48.9 us
    pallas_call x1, Pallas kernels, finish(): pl.pallas_call(finish_kernel, out_shape=jax.ShapeDtypeStruct((n_seqs, d_m...  42.3 us
    pallas_call x1, Pallas kernels, project(): pl.pallas_call(functools.partial(project_kernel, cfg), out_shape=(jax.Sha...  18.8 us

profile of v7, /device:TPU:0, one launch (start us, length us, event | category | flops | bytes accessed | tf_op | source)
XLA Modules:
  0.0 113.3 jit_solution(10473312387308983945)
XLA Ops:
  0.6 0.7 convert_add_fusion.small_ref
  1.4 0.0 copy-start.1
  1.4 1.0 copy-done.1
  2.4 0.0 copy-start
  2.4 0.0 copy-start.2
  2.4 18.8 %project.1 = (bf16[32,64,640]{2,1,0:T(8,128)(2,1)S(1)}, f32[32,640]{1,0:T(8,128)S(1)}) custom-call(f32[2176]{0:T(1024)S(1)} %convert_add_fusion.small_ref, bf16[32,7168]{1,0:T(8,128)(2,1)S(1)} %copy-done.1, bf16[7168,1536]{1,0:T(8,128)(2,1)} %w_dq.1, bf16[576,7168]{1,0:T(8,128)(2,1)} %bitcast.4, bf16[1536,12288]{1,0:T(8,128)(2,1)} %w_uq.1, ...), custom_call_target="tpu_custom_call" | custom-call | tf_op jit(solution)/shard_map/project/pallas_call | solution.py:196
  21.2 0.0 copy-done
  21.2 0.0 copy-done.2
  21.2 48.9 %attend.1 = (bf16[32,2048,512]{2,1,0:T(8,128)(2,1)}, bf16[32,64,2048]{2,1,0:T(8,128)(2,1)}, f32[8,2,17,8,512]{4,3,2,1,0:T(8,128)S(1)}, bf16[32,576]{1,0:T(8,128)(2,1)}) custom-call(s32[32]{0:T(128)S(1)} %copy-done.2, bf16[32,64,640]{2,1,0:T(8,128)(2,1)S(1)} %get-tuple-element.10.q_ref, f32[32,640]{1,0:T(8,128)S(1)} %get-tuple-element.11.kvn_ref, ...), custom_call_target="tpu_custom_call" | custom-call | tf_op jit(solution)/shard_map/attend/pallas_call | solution.py:317
  70.2 42.3 %finish.1 = f32[32,7168]{1,0:T(8,128)S(1)} custom-call(f32[8,2,17,8,512]{4,3,2,1,0:T(8,128)S(1)} %get-tuple-element.12.terms, bf16[64,128,512]{2,1,0:T(8,128)(2,1)} %w_uv.1, bf16[8192,7168]{1,0:T(8,128)(2,1)} %w_out.1), custom_call_target="tpu_custom_call" | custom-call | tf_op jit(solution)/shard_map/finish/pallas_call | solution.py:523
  112.5 0.8 convert_element_type.19
Async XLA Ops:
  1.4 1.0 copy-start.1
  2.4 18.9 %copy-start = (bf16[32,2048,64]{1,2,0:T(8,128)(2,1)S(1)}, bf16[32,2048,64]{1,2,0:T(8,128)(2,1)}, u32[]{:S(2)}) copy-start(bf16[32,2048,64]{1,2,0:T(8,128)(2,1)} %param.14) | copy-start | bytes 25165828
  2.4 18.9 %copy-start.2 = (s32[32]{0:T(128)S(1)}, s32[32]{0:T(128)}, u32[]{:S(2)}) copy-start(s32[32]{0:T(128)} %len_ref.1) | copy-start | bytes 388

commit v8 on v7

--- a/solution.py
+++ b/solution.py
@@ -182,7 +182,7 @@
     q_rank = w_dq.shape[1]
     rope_dim = w_dkv.shape[1] - lat_dim
     freqs = [float(f) for f in np.power(ROPE_THETA, -2.0 * np.arange(rope_dim // 2) / rope_dim).astype(np.float32)]
-    cfg = dict(n_kt=4, lat_dim=lat_dim, group=16, pitch=n_seqs + 8, in_flight=6, behind=2, freqs=freqs)
+    cfg = dict(n_kt=4, lat_dim=lat_dim, group=16, pitch=n_seqs + 8, in_flight=9, behind=2, freqs=freqs)
     n_k, n_blk = 8, 8
     dq_cols, dkv_cols = q_rank // 2, lat_dim // 2 + rope_dim
     blk = w_uq.shape[1] // 2 // n_blk

time: 113 us -> 113 us (level)
  no operation moved by 1% of the time
where the time goes in v8:
time: 113 us
  Pallas kernels  110 us (97%)
  other arithmetic  1.54 us (1%)
    pallas_call x1, Pallas kernels, attend(): pl.pallas_call(functools.partial(attend_kernel, cfg), out_shape=(jax.Shap...  48.9 us
    pallas_call x1, Pallas kernels, finish(): pl.pallas_call(finish_kernel, out_shape=jax.ShapeDtypeStruct((n_seqs, d_m...  42.3 us
    pallas_call x1, Pallas kernels, project(): pl.pallas_call(functools.partial(project_kernel, cfg), out_shape=(jax.Sha...  18.6 us

profile of v8, /device:TPU:0, one launch (start us, length us, event | category | flops | bytes accessed | tf_op | source)
XLA Modules:
  0.0 113.1 jit_solution(4861161689499772719)
XLA Ops:
  0.6 0.7 convert_add_fusion.small_ref
  1.4 0.0 copy-start.1
  1.4 1.0 copy-done.1
  2.4 0.0 copy-start
  2.4 0.0 copy-start.2
  2.4 18.6 %project.1 = (bf16[32,64,640]{2,1,0:T(8,128)(2,1)S(1)}, f32[32,640]{1,0:T(8,128)S(1)}) custom-call(f32[2176]{0:T(1024)S(1)} %convert_add_fusion.small_ref, bf16[32,7168]{1,0:T(8,128)(2,1)S(1)} %copy-done.1, bf16[7168,1536]{1,0:T(8,128)(2,1)} %w_dq.1, bf16[576,7168]{1,0:T(8,128)(2,1)} %bitcast.4, bf16[1536,12288]{1,0:T(8,128)(2,1)} %w_uq.1, ...), custom_call_target="tpu_custom_call" | custom-call | tf_op jit(solution)/shard_map/project/pallas_call | solution.py:196
  21.0 0.0 copy-done
  21.0 0.0 copy-done.2
  21.0 48.9 %attend.1 = (bf16[32,2048,512]{2,1,0:T(8,128)(2,1)}, bf16[32,64,2048]{2,1,0:T(8,128)(2,1)}, f32[8,2,17,8,512]{4,3,2,1,0:T(8,128)S(1)}, bf16[32,576]{1,0:T(8,128)(2,1)}) custom-call(s32[32]{0:T(128)S(1)} %copy-done.2, bf16[32,64,640]{2,1,0:T(8,128)(2,1)S(1)} %get-tuple-element.10.q_ref, f32[32,640]{1,0:T(8,128)S(1)} %get-tuple-element.11.kvn_ref, ...), custom_call_target="tpu_custom_call" | custom-call | tf_op jit(solution)/shard_map/attend/pallas_call | solution.py:317
  69.9 42.3 %finish.1 = f32[32,7168]{1,0:T(8,128)S(1)} custom-call(f32[8,2,17,8,512]{4,3,2,1,0:T(8,128)S(1)} %get-tuple-element.12.terms, bf16[64,128,512]{2,1,0:T(8,128)(2,1)} %w_uv.1, bf16[8192,7168]{1,0:T(8,128)(2,1)} %w_out.1), custom_call_target="tpu_custom_call" | custom-call | tf_op jit(solution)/shard_map/finish/pallas_call | solution.py:523
  112.3 0.8 convert_element_type.19
Async XLA Ops:
  1.4 1.0 copy-start.1
  2.4 18.6 %copy-start = (bf16[32,2048,64]{1,2,0:T(8,128)(2,1)S(1)}, bf16[32,2048,64]{1,2,0:T(8,128)(2,1)}, u32[]{:S(2)}) copy-start(bf16[32,2048,64]{1,2,0:T(8,128)(2,1)} %param.14) | copy-start | bytes 25165828
  2.4 18.6 %copy-start.2 = (s32[32]{0:T(128)S(1)}, s32[32]{0:T(128)}, u32[]{:S(2)}) copy-start(s32[32]{0:T(128)} %len_ref.1) | copy-start | bytes 388
